TPU v7x, 512 devices: a whole 4x4x16 slice. The times are simulated.
512 devices in a mesh: dp: 16 (over z_lo, x), block: 32 (over z_hi, y, core).
Axes of the slice: x: 4, y: 4, z: 16 (z_hi: 4, z_lo: 4; z = z_hi * 4 + z_lo), core: 2. Of those that a mesh axis runs over, the one named last changes fastest.
Arguments:
- positions: float32 [3, 131072], P(None, ('dp', 'block')), may hold values from -4 to 4
- neighbours: int32 [16, 131072], P(None, ('dp', 'block')), may hold values from 0 to 32
- atom_species: int32 [131072], P(('dp', 'block')), may hold values from 0 to 3
- tagged_atom: int32 [4096], P(('dp', 'block')), may hold values from 0 to 31
- observed_in: int32 [4096], P(('dp', 'block')), may hold values from 0 to 3
- targets: float32 [64], replicated, may hold values from -3 to 3
- noise_level: float32 [64], replicated, may hold values from 0.1 to 1
- embed_scale: float32 [4, 128], replicated, may hold values from -4 to 4
- embed_shift: float32 [4, 128], replicated, may hold values from -3 to 3
- first_weight: float32 [128, 256], replicated, may hold values from -1.5 to 1.5
- first_bias: float32 [256], replicated, may hold values from -3 to 3
- middle_weight: float32 [256, 256], replicated, may hold values from -0.375 to 0.375
- middle_bias: float32 [256], replicated, may hold values from -3 to 3
- energy_weight: float32 [4, 256], replicated, may hold values from -0.375 to 0.375
- covariance: float32 [32, 2048, 2048], P('block', 'dp'), as said below
Outputs:
- new_weights: float32 [32, 2048], P('block', 'dp')
- new_covariance: float32 [32, 2048, 2048], P('block', 'dp')
Inputs may be any that keep to these rules, and one draw needn't show every extreme that they name: `neighbours`: a value of 32 marks an empty slot; any other value counts an atom of the same structure. `tagged_atom`: counted within the structure. `observed_in`: the observation is counted within the structure's group. `covariance`: every block is symmetric and positive definite.
All inputs are finite; a program needn't handle non-finite values.
Results may differ from a plain program's by a relative error of at most 0.0003.
Values sent between devices are 32-bit elements; how exact they have to be, the bound alone decides.
No kernel may reach another device: no remote copies, remote signals or barrier semaphores. Data moves between devices by JAX's collectives and lax.ppermute only.
A program may use at most 64 MiB of HBM per device.

v0:
```python
import functools

import jax
import jax.numpy as jnp
import numpy as np
from jax import lax
from jax.sharding import Mesh
from jax.sharding import PartitionSpec as P

OBS = 64
DP = ("dp_0", "dp_1")
BLOCK = ("block_0", "block_1", "block_2")
DP_BLOCK = ("dp_0", "dp_1", "block_0", "block_1", "block_2")


radial_width = 4.0
forgetting = 0.98
highest = lax.Precision.HIGHEST


def by_axis(array, axes):
    return functools.reduce(lax.psum, axes, array)


def in_blocks(array, dim, peers):
    before, after = (array.shape[:dim], array.shape[dim + 1 :])
    return jnp.moveaxis(array.reshape(*before, peers, -1, *after), dim, 0)


def summed_on_arrival(array, axis, dim):
    tiles = in_blocks(array, dim, lax.axis_size(axis))
    arrived = lax.all_to_all(tiles, axis, split_axis=0, concat_axis=0, tiled=True)
    return arrived.sum(axis=0)


def joined_along(tiles, dim):
    lengths = list(tiles.shape[1:])
    lengths[dim] *= tiles.shape[0]
    return jnp.moveaxis(tiles, 0, dim).reshape(lengths)


def gather_in_order(array, axes, turns):
    tiles = array[None]
    for k in turns:
        tiles = lax.all_gather(tiles, axes[k], axis=0, tiled=True)
    carried = [lax.axis_size(axes[k]) for k in reversed(turns)]
    tiles = tiles.reshape(*carried, *array.shape)
    turned = sorted(range(len(turns)), key=lambda place: turns[len(turns) - 1 - place])
    return tiles.transpose(*turned, *range(len(turns), tiles.ndim)).reshape(-1, *array.shape)


def gathered_by_axis(array, axes, turns, dim):
    return joined_along(gather_in_order(array, axes, turns), dim)


def observations(
    window,
    positions,
    neighbours,
    atom_species,
    tagged_atom,
    observed_in,
    embed_scale,
    embed_shift,
    first_weight,
    first_bias,
    middle_weight,
    middle_bias,
    energy_weight,
    obs_count,
    weighting,
):
    atom_total = positions.shape[1]
    struct_total = tagged_atom.shape[0]
    struct_size = atom_total // struct_total
    species_count = embed_scale.shape[0]
    slot_count = neighbours.shape[0]
    struct_start = jnp.arange(atom_total, dtype=jnp.int32) // struct_size * struct_size
    live_slot = (neighbours < struct_size).astype(jnp.float32)
    neighbour_at = struct_start[None, :] + jnp.minimum(neighbours, struct_size - 1)
    near_species = atom_species[neighbour_at]
    species_range = jnp.arange(species_count, dtype=jnp.int32)
    species_table = (near_species[None, :, :] == species_range[:, None, None]).astype(jnp.float32)
    edge_scale = jnp.einsum("se,ska->eka", embed_scale, species_table, precision=highest)
    edge_shift = jnp.einsum("se,ska->eka", embed_shift, species_table, precision=highest)
    own_species = (atom_species[None, :] == species_range[:, None]).astype(jnp.float32)
    readout = jnp.dot(energy_weight.T, own_species, precision=highest)
    remainder = middle_weight[window.shape[0] :]

    def site_energy(coords, middle):
        displace = coords[:, neighbour_at] - coords[:, None, :]
        distance_sq = jnp.sum(displace * displace, axis=0)
        radial = jnp.exp(-distance_sq / radial_width) * live_slot
        embedded = jnp.tanh(radial[None] * edge_scale + edge_shift)
        descriptor = jnp.sum(radial[None] * embedded, axis=1) / slot_count
        first_layer = jnp.tanh(
            jnp.dot(first_weight.T, descriptor, precision=highest) + first_bias[:, None]
        )
        second_layer = jnp.tanh(
            jnp.dot(middle.T, first_layer, precision=highest) + middle_bias[:, None]
        )
        return jnp.sum(readout * second_layer, axis=0)

    def predict(window_part):
        middle = jnp.concatenate([window_part, remainder], axis=0)
        energies, pullback = jax.vjp(lambda coords: site_energy(coords, middle), positions)
        forces = -pullback(jnp.ones_like(energies))[0]
        per_struct = jnp.sum(energies.reshape(struct_total, struct_size), axis=1) / struct_size
        tag_table = (
            tagged_atom[:, None] == jnp.arange(struct_size, dtype=jnp.int32)[None, :]
        ).astype(jnp.float32)
        picked = jnp.sum(forces.reshape(3, struct_total, struct_size) * tag_table[None], axis=2)
        values = jnp.concatenate([per_struct[None, :], picked], axis=0)
        value_rows = values[np.arange(obs_count) % 4]
        chosen = (observed_in[None, :] == jnp.arange(obs_count, dtype=jnp.int32)[:, None]).astype(
            jnp.float32
        )
        return jnp.sum(chosen * value_rows, axis=1) * weighting

    predicted, pullback = jax.vjp(predict, window)
    basis = jnp.eye(obs_count, dtype=predicted.dtype)
    jacobian = lax.map(lambda row: pullback(row)[0], basis)
    return (predicted, jacobian)


def local(
    positions,
    neighbours,
    atom_species,
    tagged_atom,
    observed_in,
    targets,
    noise_level,
    embed_scale,
    embed_shift,
    first_weight,
    first_bias,
    middle_weight,
    middle_bias,
    energy_weight,
    covariance,
):
    group_count = lax.axis_size(DP)
    block_count = lax.axis_size(BLOCK)
    block_order = covariance.shape[2]
    row_share = covariance.shape[1]
    obs_group = OBS // group_count
    weighting = OBS / (tagged_atom.shape[0] * group_count * block_count)
    predicted_here, jacobian_here = observations(
        middle_weight,
        positions,
        neighbours,
        atom_species,
        tagged_atom,
        observed_in,
        embed_scale,
        embed_shift,
        first_weight,
        first_bias,
        middle_weight,
        middle_bias,
        energy_weight,
        obs_group,
        weighting,
    )
    spread = jnp.zeros((OBS,), jnp.float32)
    spread = lax.dynamic_update_slice_in_dim(
        spread, predicted_here, lax.axis_index(DP) * obs_group, 0
    )
    predicted = by_axis(spread, DP_BLOCK)
    jacobian_block = summed_on_arrival(jacobian_here, BLOCK, 1)
    jacobian = gathered_by_axis(jacobian_block.reshape(obs_group, block_order), DP, (0, 1), 0)
    cov_rows = covariance[0]
    product = jnp.dot(cov_rows, jacobian.T, precision=highest)
    columns = lax.dynamic_slice_in_dim(jacobian, lax.axis_index(DP) * row_share, row_share, 1)
    partial_value = jnp.dot(columns, product, precision=highest)
    gram_sum = by_axis(partial_value, DP_BLOCK)
    gram_sum = 0.5 * (gram_sum + gram_sum.T) + jnp.diag(noise_level)
    factor = jnp.linalg.cholesky(gram_sum)
    inverse = jax.scipy.linalg.cho_solve((factor, True), jnp.eye(OBS, dtype=jnp.float32))
    gain_rows = jnp.dot(product, inverse, precision=highest)
    gains_all = gathered_by_axis(gain_rows, DP, (0, 1), 0)
    update = jnp.dot(product, gains_all.T, precision=highest)
    innovation = targets - predicted
    block_window = lax.dynamic_slice_in_dim(
        middle_weight.reshape(block_count, block_order), lax.axis_index(BLOCK), 1, 0
    )
    window_rows = lax.dynamic_slice_in_dim(
        block_window, lax.axis_index(DP) * row_share, row_share, 1
    )
    new_weights = window_rows + jnp.dot(gain_rows, innovation, precision=highest)[None, :]
    new_covariance = ((cov_rows - update) / forgetting)[None]
    return (new_weights, new_covariance)


def solution(mesh):
    finer = Mesh(
        mesh.devices.reshape(4, 4, 4, 4, 2), ("dp_0", "dp_1", "block_0", "block_1", "block_2")
    )
    placed = (
        P(None, DP_BLOCK),
        P(None, DP_BLOCK),
        P(DP_BLOCK),
        P(DP_BLOCK),
        P(DP_BLOCK),
        P(),
        P(),
        P(),
        P(),
        P(),
        P(),
        P(),
        P(),
        P(),
        P(BLOCK, DP, None),
    )
    return jax.shard_map(
        local,
        mesh=finer,
        in_specs=placed,
        out_specs=(P(BLOCK, DP), P(BLOCK, DP, None)),
        check_vma=False,
    )
```

profile of v0, /device:TPU:1, one launch (start us, length us, event | category | flops | bytes accessed | tf_op | source)
XLA Modules:
  0.0 410.4 jit_solution(4071571019133025866)
XLA Ops:
  2.8 14.1 %gather_fusion.1 = f32[4096,3]{1,0:T(8,128)} fusion(f32[3,256]{0,1:T(8,128)S(1)} %copy.124, s32[4096]{0:T(1024)S(1)} %broadcast_clamp_fusion.1), kind=kCustom, calls=%fused_computation.1 | custom fusion | bytes 114688 | tf_op jit(solution)/shard_map/jvp(jvp())/gather | solution.py:91
  19.8 25.9 %gather_fusion.2 = s32[4096]{0:T(1024)S(1)} fusion(s32[256]{0:T(256)S(1)} %copy-done.1, s32[4096]{0:T(1024)S(1)} %broadcast_clamp_fusion.1), kind=kCustom, calls=%fused_computation.2 | custom fusion | bytes 49152 | tf_op jit(solution)/shard_map/gather | solution.py:81
  46.8 2.7 multiply_reduce_fusion.3
  55.0 4.2 %copy.131 = f32[128,16,256]{2,1,0:T(8,128)} copy(f32[128,16,256]{2,0,1:T(8,128)} %copy-done.4) | data formatting | bytes 4194304
  65.3 4.3 %copy.130 = f32[128,16,256]{2,1,0:T(8,128)} copy(f32[128,16,256]{2,0,1:T(8,128)} %get-tuple-element.359) | data formatting | bytes 4194304
  77.5 111.7 %while.11 = (s32[]{:T(128)}, f32[4,256,256]{2,1,0:T(8,128)}, f32[4,4]{1,0:T(4,128)}, s32[16,256,1]{1,2,0:T(1,128)}, f32[3,16,256]{0,2,1:T(8,128)S(1)}, /*index=5...) while((s32[]{:T(128)}, f32[4,256,256]{2,1,0:T(8,128)}, ...), condition=%wide.region_6.7_spmd.clone, body=%wide.region_2.6_spmd.clone.sunk | while | flops 708315264 | bytes 29019484 | solution.py:122
  80.7 15.4 %gather_fusion = f32[4096,3]{1,0:T(8,128)} fusion(f32[3,256]{0,1:T(8,128)S(1)} %get-tuple-element.492, s32[4096]{0:T(1024)} %broadcast_clamp_fusion.3), kind=kCustom, calls=%fused_computation.clone.clone.1 | custom fusion | bytes 114688 | tf_op jit(solution)/shard_map/while/body/eval_jaxpr/transpose(jvp(transpose(jvp())))/gather | solution.py:91
  108.6 15.4 %gather_fusion = f32[4096,3]{1,0:T(8,128)} fusion(f32[3,256]{0,1:T(8,128)S(1)} %get-tuple-element.492, s32[4096]{0:T(1024)} %broadcast_clamp_fusion.3), kind=kCustom, calls=%fused_computation.clone.clone.1 | custom fusion | bytes 114688 | tf_op jit(solution)/shard_map/while/body/eval_jaxpr/transpose(jvp(transpose(jvp())))/gather | solution.py:91
  136.5 15.4 %gather_fusion = f32[4096,3]{1,0:T(8,128)} fusion(f32[3,256]{0,1:T(8,128)S(1)} %get-tuple-element.492, s32[4096]{0:T(1024)} %broadcast_clamp_fusion.3), kind=kCustom, calls=%fused_computation.clone.clone.1 | custom fusion | bytes 114688 | tf_op jit(solution)/shard_map/while/body/eval_jaxpr/transpose(jvp(transpose(jvp())))/gather | solution.py:91
  164.4 15.4 %gather_fusion = f32[4096,3]{1,0:T(8,128)} fusion(f32[3,256]{0,1:T(8,128)S(1)} %get-tuple-element.492, s32[4096]{0:T(1024)} %broadcast_clamp_fusion.3), kind=kCustom, calls=%fused_computation.clone.clone.1 | custom fusion | bytes 114688 | tf_op jit(solution)/shard_map/while/body/eval_jaxpr/transpose(jvp(transpose(jvp())))/gather | solution.py:91
  191.6 19.4 %all-to-all-start = ((f32[32,4,8,256]{3,2,1,0:T(8,128)}), f32[32,4,8,256]{3,2,1,0:T(8,128)S(1)}, u32[]{:S(2)}, u32[]{:S(2)}) async-start(f32[32,4,8,256]{3,2,1,0:T(8,128)} %copy.135), calls=%async_computation | async-start | bytes 2097152 | tf_op jit(solution)/shard_map/all_to_all | solution.py:32
  213.5 22.7 %scatter_fusion = f32[3,256]{0,1:T(8,128)S(1)} fusion(f32[3,256]{0,1:T(8,128)S(1)} %neg.22, s32[4096]{0:T(1024)S(1)} %bitcast.193, f32[4096,3]{1,0:T(8,128)} %bitcast.185), kind=kCustom, calls=%fused_computation.5 | custom fusion | flops 12288 | bytes 163840 | tf_op jit(solution)/shard_map/jvp(transpose(jvp()))/scatter-add | solution.py:91
  237.6 26.1 %all-to-all-done = f32[32,4,8,256]{3,2,1,0:T(8,128)S(1)} async-done(((f32[32,4,8,256]{3,2,1,0:T(8,128)}), f32[32,4,8,256]{3,2,1,0:T(8,128)S(1)}, u32[]{:S(2)}, u32[]{:S(2)}) %all-to-all-start) | async-done | bytes 1048608 | tf_op jit(solution)/shard_map/all_to_all | solution.py:32
  263.8 12.5 %all_gather.12 = f32[4,4,2048]{2,1,0:T(4,128)S(1)} all-gather(f32[1,4,2048]{2,1,0:T(4,128)S(1)} %broadcast_in_dim_reshape.3), channel_id=1, replica_groups=mesh['dp_0'=4,'dp_1'=4,'block_0'=4,'block_1'=4,'block_2'=2] {'dp_0'}, dimensions={0}, use_global_device_ids=true | all-gather | bytes 163840 | tf_op jit(solution)/shard_map/all_gather | solution.py:45
  276.3 10.4 %all_gather.13 = f32[16,4,2048]{2,1,0:T(4,128)S(1)} all-gather(f32[4,4,2048]{2,1,0:T(4,128)S(1)} %all_gather.12), channel_id=1, replica_groups=mesh['dp_0'=4,'dp_1'=4,'block_0'=4,'block_1'=4,'block_2'=2] {'dp_1'}, dimensions={0}, use_global_device_ids=true | all-gather | bytes 655360 | tf_op jit(solution)/shard_map/all_gather | solution.py:45
  288.3 13.8 %all-reduce.3 = (f32[64,64]{0,1:T(8,128)S(1)}, f32[64]{0:T(128)S(1)}) all-reduce(f32[64,64]{0,1:T(8,128)S(1)} %fusion.46, f32[64]{0:T(128)S(1)} %multiply_dynamic-update-slice_fusion), channel_id=1, replica_groups=mesh['dp_0'=4,'dp_1'=4,'block_0'=4,'block_1'=4,'block_2'=2] {'dp_0'}, use_global_device_ids=true, to_apply=%region_8.9 | all-reduce | flops 4160 | bytes 33280 | tf_op jit(solution)/shard_map/psum | solution.py:22
  302.1 14.2 %all-reduce.2 = (f32[64,64]{0,1:T(8,128)S(1)}, f32[64]{0:T(128)S(1)}) all-reduce(f32[64,64]{0,1:T(8,128)S(1)} %get-tuple-element.339, f32[64]{0:T(128)S(1)} %get-tuple-element.340), channel_id=1, replica_groups=mesh['dp_0'=4,'dp_1'=4,'block_0'=4,'block_1'=4,'block_2'=2] {'dp_1'}, use_global_device_ids=true, to_apply=%region_9.10 | all-reduce | flops 4160 | bytes 33280 | tf_op jit(solution)/shard_map/psum | solution.py:22
  316.3 21.1 %all-reduce.1 = (f32[64,64]{0,1:T(8,128)S(1)}, f32[64]{0:T(128)S(1)}) all-reduce(f32[64,64]{0,1:T(8,128)S(1)} %get-tuple-element.337, f32[64]{0:T(128)S(1)} %get-tuple-element.338), channel_id=1, replica_groups=mesh['dp_0'=4,'dp_1'=4,'block_0'=4,'block_1'=4,'block_2'=2] {'block_0'}, use_global_device_ids=true, to_apply=%region_10.11 | all-reduce | flops 4160 | bytes 33280 | tf_op jit(solution)/shard_map/psum | solution.py:22
  337.4 11.5 %all-reduce = (f32[64,64]{0,1:T(8,128)S(1)}, f32[64]{0:T(128)S(1)}) all-reduce(f32[64,64]{0,1:T(8,128)S(1)} %get-tuple-element.335, f32[64]{0:T(128)S(1)} %get-tuple-element.336), channel_id=1, replica_groups=mesh['dp_0'=4,'dp_1'=4,'block_0'=4,'block_1'=4,'block_2'=2] {'block_1'}, use_global_device_ids=true, to_apply=%region_11.12 | all-reduce | flops 4160 | bytes 33280 | tf_op jit(solution)/shard_map/psum | solution.py:22
  348.9 22.9 %all-reduce.4 = (f32[64,64]{0,1:T(8,128)S(1)}, f32[64]{0:T(128)S(1)}) all-reduce(f32[64,64]{0,1:T(8,128)S(1)} %get-tuple-element.333, f32[64]{0:T(128)S(1)} %get-tuple-element.334), channel_id=1, replica_groups=mesh['dp_0'=4,'dp_1'=4,'block_0'=4,'block_1'=4,'block_2'=2] {'block_2'}, use_global_device_ids=true, to_apply=%region_12.13 | all-reduce | flops 4160 | bytes 33280 | tf_op jit(solution)/shard_map/psum | solution.py:22
  372.0 5.8 %cholesky.17 = f32[64,64]{1,0:T(8,128)S(1)} custom-call(f32[64,64]{1,0:T(8,128)S(1)} %fusion.43), custom_call_target="Cholesky" | custom-call | tf_op jit(solution)/shard_map/jit(cholesky)/cholesky | solution.py:179
  379.2 4.9 %custom-call.10 = f32[1,64,64]{1,2,0:T(8,128)S(1)} custom-call(f32[1,64,64]{2,1,0:T(8,128)S(1)} %fusion.38), custom_call_target="InvertDiagBlocksLowerTriangular" | custom-call | tf_op jit(solution)/shard_map/jit(_cho_solve)/triangular_solve | solution.py:180
  384.7 10.5 %all-gather = f32[512,64]{0,1:T(8,128)S(1)} all-gather(f32[128,64]{0,1:T(8,128)S(1)} %fusion.64), channel_id=2, replica_groups=mesh['dp_0'=4,'dp_1'=4,'block_0'=4,'block_1'=4,'block_2'=2] {'dp_0'}, dimensions={0}, use_global_device_ids=true | all-gather | bytes 163840 | tf_op jit(solution)/shard_map/all_gather | solution.py:45
  395.2 11.2 %all_gather.15 = f32[16,128,64]{1,2,0:T(8,128)S(1)} all-gather(f32[4,128,64]{1,2,0:T(8,128)S(1)} %copy_bitcast_fusion), channel_id=1, replica_groups=mesh['dp_0'=4,'dp_1'=4,'block_0'=4,'block_1'=4,'block_2'=2] {'dp_1'}, dimensions={0}, use_global_device_ids=true | all-gather | bytes 655360 | tf_op jit(solution)/shard_map/all_gather | solution.py:45
  (255 shorter events, 89.2 us)
Async XLA Ops:
  0.6 49.8 %copy-start = (f32[4,256]{1,0:T(4,128)S(1)}, f32[4,256]{1,0:T(4,128)}, u32[]{:S(2)}) copy-start(f32[4,256]{1,0:T(4,128)} %param.32) | copy-start | bytes 12292
  16.9 2.9 copy-start.1
  19.8 27.0 %copy-start.16 = (f32[16,256]{1,0:T(8,128)}, f32[16,256]{1,0:T(8,128)S(1)}, u32[]{:S(2)}) copy-start(f32[16,256]{1,0:T(8,128)S(1)} %get-tuple-element.347) | copy-start | bytes 49156
  19.8 25.9 %copy-start.30 = (f32[4,128]{1,0:T(4,128)S(1)}, f32[4,128]{1,0:T(4,128)}, u32[]{:S(2)}) copy-start(f32[4,128]{1,0:T(4,128)} %param.26) | copy-start | bytes 6148
  46.8 3.2 copy-start.8
  46.8 3.2 copy-start.33
  55.0 4.8 %copy-start.9 = (f32[256,256]{1,0:T(8,128)S(1)}, f32[256,256]{1,0:T(8,128)}, u32[]{:S(2)}) copy-start(f32[256,256]{1,0:T(8,128)} %param.30) | copy-start | bytes 786436
  64.2 5.3 %copy-start.17 = (f32[16,256]{1,0:T(8,128)S(1)}, f32[16,256]{1,0:T(8,128)}, u32[]{:S(2)}) copy-start(f32[16,256]{1,0:T(8,128)} %copy-done.16) | copy-start | bytes 49156
  65.3 4.3 %copy-start.5 = (f32[128,16,256]{2,0,1:T(8,128)S(1)}, f32[128,16,256]{2,0,1:T(8,128)}, u32[]{:S(2)}) copy-start(f32[128,16,256]{2,0,1:T(8,128)} %copy-done.4) | copy-start | bytes 6291460
  65.3 4.3 %copy-start.6 = (f32[128,16,256]{2,0,1:T(8,128)S(1)}, f32[128,16,256]{2,0,1:T(8,128)}, u32[]{:S(2)}) copy-start(f32[128,16,256]{2,0,1:T(8,128)} %get-tuple-element.359) | copy-start | bytes 6291460
  70.8 6.7 %copy-start.26 = (s32[8]{0:T(128)S(1)}, s32[8]{0:T(128)}, u32[]{:S(2)}) copy-start(s32[8]{0:T(128)} %param.22) | copy-start | bytes 100
  96.1 2.9 copy-start.3
  101.6 3.8 copy-start.27
  129.5 3.8 copy-start.27
  151.9 2.9 copy-start.3
  157.5 3.8 copy-start.27
  185.4 3.8 copy-start.27
  189.2 21.8 %copy-start.10 = (f32[256,256]{1,0:T(8,128)S(1)}, f32[256,256]{1,0:T(8,128)}, u32[]{:S(2)}) copy-start(f32[256,256]{1,0:T(8,128)} %param.30) | copy-start | bytes 786436
  189.2 22.5 %copy-start.25 = (f32[16,256]{1,0:T(8,128)S(1)}, f32[16,256]{1,0:T(8,128)}, u32[]{:S(2)}) copy-start(f32[16,256]{1,0:T(8,128)} %get-tuple-element.356) | copy-start | bytes 49156
  191.6 72.1 %all-to-all-start = ((f32[32,4,8,256]{3,2,1,0:T(8,128)}), f32[32,4,8,256]{3,2,1,0:T(8,128)S(1)}, u32[]{:S(2)}, u32[]{:S(2)}) async-start(f32[32,4,8,256]{3,2,1,0:T(8,128)} %copy.135), calls=%async_computation | async-start | bytes 2097152 | tf_op jit(solution)/shard_map/all_to_all | solution.py:32
  211.8 24.8 %copy-start.29 = (f32[256]{0:T(256)S(1)}, f32[256]{0:T(256)}, u32[]{:S(2)}) copy-start(f32[256]{0:T(256)} %get-tuple-element.352) | copy-start | bytes 3076
  211.8 25.6 %copy-start.28 = (s32[8]{0:T(128)S(1)}, s32[8]{0:T(128)}, u32[]{:S(2)}) copy-start(s32[8]{0:T(128)} %get-tuple-element.589) | copy-start | bytes 100
  236.5 50.5 %copy-start.13 = (f32[1,128,2048]{2,1,0:T(8,128)S(1)}, f32[1,128,2048]{2,1,0:T(8,128)}, u32[]{:S(2)}) copy-start(f32[1,128,2048]{2,1,0:T(8,128)} %param.33) | copy-start | bytes 3145732
  286.7 85.1 %copy-start.34 = (f32[64]{0:T(128)S(1)}, f32[64]{0:T(128)}, u32[]{:S(2)}) copy-start(f32[64]{0:T(128)} %param.25) | copy-start | bytes 772
  (34 other events, 78.0 us)
where the time goes:
time: 415 us; the launch traced here: 410 us
  local copies, waits for them, and re-layouts  129 us (31%)
  blocking collectives  128 us (31%)
  other arithmetic  76.8 us (19%)
  matrix products  29.2 us (7%)
  waiting for transfers between devices  26.1 us (6%)
  starting transfers between devices  19.4 us (5%)
    psum x5, blocking collectives, by_axis(): return functools.reduce(lax.psum, axes, array)  83.4 us
    gather x5, local copies, waits for them, and re-layouts, site_energy(): displace = coords[:, neighbour_at] - coords[:, None, :]  75.7 us
    all_gather x4, blocking collectives, gather_in_order(): tiles = lax.all_gather(tiles, axes[k], axis=0, tiled=True)  44.6 us
    all_to_all x1, waiting for transfers between devices, summed_on_arrival(): lax.all_to_all(tiles, axis, split_axis=0, concat_axis=0, tiled=True)  26.1 us
    gather x2, local copies, waits for them, and re-layouts, observations(): near_species = atom_species[neighbour_at]  25.9 us
    scatter-add x1, other arithmetic, site_energy(): displace = coords[:, neighbour_at] - coords[:, None, :]  22.7 us
    all_to_all x1, starting transfers between devices, summed_on_arrival(): lax.all_to_all(tiles, axis, split_axis=0, concat_axis=0, tiled=True)  19.4 us
    unnamed x67, local copies, waits for them, and re-layouts  17.6 us
  transfers between devices with their start and end apart: 1, of which 1 were waited for; matrix products, arithmetic and copies ran while one was open for 6% of the time, Pallas kernels for 0%

commit v1 on v0

v1 whole, which is shorter than its diff:
```python
import functools

import jax
import jax.numpy as jnp
from jax import lax
from jax.experimental import pallas as pl
from jax.experimental.pallas import tpu as pltpu
from jax.sharding import Mesh
from jax.sharding import PartitionSpec as P

OBS = 64
GROUPS = 16
OBS_DP = 4
STRUCT = 32
LOCAL_STRUCTS = 8
ATOMS = 256
LANES = 128
HID = 256
EMB = 128
SLOTS = 16
ORDER = 2048
ROWS = 128
DP = ("dp_0", "dp_1")
BLOCK = ("block_0", "block_1", "block_2")
DP_BLOCK = ("dp_0", "dp_1", "block_0", "block_1", "block_2")

radial_width = 4.0
forgetting = 0.98
highest = lax.Precision.HIGHEST

VMEM = pl.BlockSpec(memory_space=pltpu.VMEM)
SMEM = pl.BlockSpec(memory_space=pltpu.SMEM)


def contract(lhs, rhs, over):
    return lax.dot_general(
        lhs, rhs, ((over[:1], over[1:]), ((), ())), precision=highest, preferred_element_type=jnp.float32
    )


def along_lanes(row, at):
    return jnp.take_along_axis(
        jnp.broadcast_to(row, at.shape), at, axis=1, mode="promise_in_bounds"
    )


def jacobian_kernel(
    place,
    tagged,
    observed,
    positions,
    neighbours,
    species,
    scale,
    shift,
    first_weight,
    first_bias,
    middle_weight,
    middle_bias,
    energy_weight,
    mine,
    theirs,
    predicted,
    window,
    tables,
    descriptor,
    forward,
    heads,
    jacobian,
    weighting,
):
    core, block, group = place[0], place[1], place[2]
    for kind, table in enumerate((scale, shift)):
        columns = table[:].T
        for s in range(4):
            tables[kind * 4 + s] = jnp.broadcast_to(columns[:, s : s + 1], (EMB, LANES))
    lane = lax.broadcasted_iota(jnp.int32, (SLOTS, LANES), 1)
    for half in range(2):
        lanes = slice(half * LANES, (half + 1) * LANES)
        tag = jnp.zeros((SLOTS, LANES), jnp.int32)
        part = jnp.zeros((SLOTS, LANES), jnp.int32)
        for s in range(4):
            here = lane // STRUCT == s
            tag = jnp.where(here, tagged[half * 4 + s], tag)
            part = jnp.where(here, observed[half * 4 + s], part)
        listed = neighbours[:, lanes]
        within = jnp.minimum(listed, STRUCT - 1)
        at = lane // STRUCT * STRUCT + within
        distance_sq = jnp.zeros((SLOTS, LANES), jnp.float32)
        chosen = jnp.zeros((SLOTS, LANES), jnp.float32)
        for c in range(3):
            row = positions[c : c + 1, lanes]
            displace = along_lanes(row, at) - row
            distance_sq = distance_sq + displace * displace
            chosen = jnp.where(part == c + 1, displace, chosen)
        radial = jnp.exp(-distance_sq / radial_width) * (listed < STRUCT).astype(jnp.float32)
        moved = (within == tag).astype(jnp.float32) - (lane % STRUCT == tag).astype(jnp.float32)
        radial_dot = radial * (-2.0 / radial_width) * chosen * moved
        near = along_lanes(species[:, lanes], at)
        odd = (near & 1) == 1
        upper = near >= 2

        def embed(step, carry, half=half, radial=radial, radial_dot=radial_dot, odd=odd, upper=upper):
            start = pl.multiple_of(step * 16, 16)
            rows = pl.ds(start, 16)
            held = [tables[n, rows, :] for n in range(8)]
            total = jnp.zeros((16, LANES), jnp.float32)
            tangent = jnp.zeros((16, LANES), jnp.float32)
            for k in range(SLOTS):
                r = jnp.broadcast_to(radial[k : k + 1], (16, LANES))
                r_dot = jnp.broadcast_to(radial_dot[k : k + 1], (16, LANES))
                is_odd = jnp.broadcast_to(odd[k : k + 1], (16, LANES))
                is_upper = jnp.broadcast_to(upper[k : k + 1], (16, LANES))
                slope = jnp.where(
                    is_upper,
                    jnp.where(is_odd, held[3], held[2]),
                    jnp.where(is_odd, held[1], held[0]),
                )
                offset = jnp.where(
                    is_upper,
                    jnp.where(is_odd, held[7], held[6]),
                    jnp.where(is_odd, held[5], held[4]),
                )
                steep = r * slope
                bent = jnp.tanh(steep + offset)
                total = total + r * bent
                tangent = tangent + r_dot * (bent + steep * (1.0 - bent * bent))
            descriptor[rows, half * LANES : (half + 1) * LANES] = total / SLOTS
            descriptor[rows, ATOMS + half * LANES : ATOMS + (half + 1) * LANES] = tangent / SLOTS
            return carry

        lax.fori_loop(0, EMB // 16, embed, 0)

    inner = contract(descriptor[:], first_weight[:], (0, 0))
    first = jnp.tanh(inner[:ATOMS] + first_bias[:])
    forward[:ATOMS] = first
    forward[ATOMS:] = (1.0 - first * first) * inner[ATOMS:]
    outer = contract(forward[:], middle_weight[:], (1, 0))
    second = jnp.tanh(outer[:ATOMS] + middle_bias[:])
    bend = 1.0 - second * second
    second_dot = bend * outer[ATOMS:]
    own = lax.broadcasted_iota(jnp.int32, (4, ATOMS), 0) == species[:]
    readout = contract(own.astype(jnp.float32), energy_weight[:], (0, 0))
    slope = readout * bend
    slope_dot = -2.0 * readout * second * second_dot
    energy = readout * second
    force = -(readout * second_dot)
    sums = [jnp.zeros((1, HID), jnp.float32) for _ in range(OBS_DP)]
    for s in range(LOCAL_STRUCTS):
        rows = slice(s * STRUCT, (s + 1) * STRUCT)
        q = observed[s]
        is_energy = q == 0
        direct = jnp.where(is_energy, slope[rows] * (weighting / STRUCT), slope_dot[rows] * -weighting)
        through = slope[rows] * -weighting
        value = jnp.sum(
            jnp.where(is_energy, energy[rows] * (weighting / STRUCT), force[rows] * weighting),
            axis=0,
            keepdims=True,
        )
        for o in range(OBS_DP):
            columns = slice(o * HID, (o + 1) * HID)
            heads[s * STRUCT : (s + 1) * STRUCT, columns] = jnp.where(q == o, direct, 0.0)
            heads[ATOMS + s * STRUCT : ATOMS + (s + 1) * STRUCT, columns] = jnp.where(
                q == o, through, 0.0
            )
            sums[o] = sums[o] + jnp.where(q == o, value, 0.0)
    predicted[:] = jnp.zeros((8, LANES), jnp.float32)
    for o in range(OBS_DP):
        predicted[o : o + 1, :] = sums[o][:, :LANES] + sums[o][:, LANES:]
    jacobian[:] = contract(forward[:], heads[:], (0, 0))
    for y in range(4):
        for z in range(4):
            pair = (z * 8 + y * 2) * 8
            kept = pl.multiple_of(pair + core * 8, 8)
            sent = pl.multiple_of(pair + (1 - core) * 8, 8)
            mine[y, z] = jacobian[pl.ds(kept, 8), :]
            theirs[y, z] = jacobian[pl.ds(sent, 8), :]
    line = middle_weight[pl.ds(block * 8 + group // 2, 1), :]
    window[:] = jnp.where(group % 2 == 0, line[:, :LANES], line[:, LANES:])


def product_kernel(gathered, covariance, predicted, columns, sent):
    for i in range(8):
        for q in range(OBS_DP):
            columns[q * GROUPS : (q + 1) * GROUPS, i * HID : (i + 1) * HID] = gathered[
                :, i, q * HID : (q + 1) * HID
            ]
    product = contract(columns[:], covariance[0], (1, 1))
    for d in range(GROUPS):
        sent[d, :OBS] = product
        sent[d, OBS:] = predicted[:]


def gram_kernel(columns, products, sent):
    gram = jnp.zeros((OBS, OBS), jnp.float32)
    for d in range(GROUPS):
        gram = gram + contract(columns[:, d * ROWS : (d + 1) * ROWS], products[d, :OBS], (1, 1))
    half = OBS // 2
    values = jnp.sum(
        jnp.concatenate([products[:, OBS + q, :] for q in range(OBS_DP)], axis=0),
        axis=1,
        keepdims=True,
    )
    packed = jnp.concatenate(
        [
            gram[:half],
            gram[half:, half:],
            values[:half],
            values[half:],
            jnp.zeros((half, half - 2), jnp.float32),
        ],
        axis=1,
    )
    for k in range(8):
        sent[k] = packed


def summed_kernel(arrived, sent):
    total = arrived[0]
    for k in range(1, 8):
        total = total + arrived[k]
    for k in range(4):
        sent[k] = total


def update_kernel(
    place, arrived, products, covariance, window, targets, noise, new_weights, new_covariance, wide
):
    group = place[2]
    half = OBS // 2
    packed = (arrived[0] + arrived[1]) + (arrived[2] + arrived[3])
    corner = packed[:, half:OBS]
    gram = jnp.concatenate(
        [
            packed[:, :OBS],
            jnp.concatenate([corner.T, packed[:, OBS : OBS + half]], axis=1),
        ],
        axis=0,
    )
    gram = 0.5 * (gram + gram.T)
    observed = jnp.concatenate([packed[:, 96:97], packed[:, 97:98]], axis=0)
    down = lax.broadcasted_iota(jnp.int32, (OBS, OBS), 0)
    across = lax.broadcasted_iota(jnp.int32, (OBS, OBS), 1)
    source = across == down % GROUPS * OBS_DP + down // GROUPS
    noise_here = jnp.sum(jnp.where(source, noise[:], 0.0), axis=1, keepdims=True)
    target_here = jnp.sum(jnp.where(source, targets[:], 0.0), axis=1, keepdims=True)
    identity = (down == across).astype(jnp.float32)
    gram = gram + jnp.where(down == across, noise_here, 0.0)
    work = jnp.concatenate([gram, identity], axis=1)
    below = lax.broadcasted_iota(jnp.int32, (OBS, 1), 0)
    pivots = jnp.ones((OBS, 1), jnp.float32)
    for k in range(OBS):
        row = work[k : k + 1, :]
        pivot = row[:, k : k + 1]
        factor = jnp.where(below > k, work[:, k : k + 1] / pivot, 0.0)
        pivots = jnp.where(below == k, pivot, pivots)
        work = work - factor * row
    root = work[:, OBS:] * lax.rsqrt(pivots)
    for d in range(GROUPS):
        wide[:, d * ROWS : (d + 1) * ROWS] = products[d, :OBS]
    own = products[group, :OBS]
    gain = contract(root, contract(root, own, (1, 0)), (0, 0))
    new_weights[:] = window[:] + jnp.sum(gain * (target_here - observed), axis=0, keepdims=True)
    new_covariance[0] = (covariance[0] - contract(gain, wide[:], (0, 0))) / forgetting


def exchanged(tiles, axes):
    return lax.all_to_all(tiles, axes, split_axis=0, concat_axis=0, tiled=True)


def local(
    positions,
    neighbours,
    atom_species,
    tagged_atom,
    observed_in,
    targets,
    noise_level,
    embed_scale,
    embed_shift,
    first_weight,
    first_bias,
    middle_weight,
    middle_bias,
    energy_weight,
    covariance,
    weighting,
):
    f32 = jnp.float32
    place = jnp.stack(
        [lax.axis_index("block_2"), lax.axis_index(BLOCK), lax.axis_index(DP)]
    ).astype(jnp.int32)
    mine, theirs, predicted, window = pl.pallas_call(
        functools.partial(jacobian_kernel, weighting=weighting),
        out_shape=(
            jax.ShapeDtypeStruct((4, 4, 8, OBS_DP * HID), f32),
            jax.ShapeDtypeStruct((4, 4, 8, OBS_DP * HID), f32),
            jax.ShapeDtypeStruct((8, LANES), f32),
            jax.ShapeDtypeStruct((1, LANES), f32),
        ),
        in_specs=[SMEM, SMEM, SMEM] + [VMEM] * 10,
        out_specs=(VMEM, VMEM, VMEM, VMEM),
        scratch_shapes=[
            pltpu.VMEM((8, EMB, LANES), f32),
            pltpu.VMEM((EMB, 2 * ATOMS), f32),
            pltpu.VMEM((2 * ATOMS, HID), f32),
            pltpu.VMEM((2 * ATOMS, OBS_DP * HID), f32),
            pltpu.VMEM((HID, OBS_DP * HID), f32),
        ],
    )(
        place,
        tagged_atom,
        observed_in,
        positions,
        neighbours,
        atom_species[None],
        embed_scale,
        embed_shift,
        first_weight,
        first_bias[None],
        middle_weight,
        middle_bias[None],
        energy_weight,
    )
    partner = mine + lax.ppermute(theirs, "block_2", [(0, 1), (1, 0)])
    across_y = jnp.sum(exchanged(partner, "block_1"), axis=0)
    across_z = jnp.sum(exchanged(across_y, "block_0"), axis=0)
    gathered = exchanged(jnp.broadcast_to(across_z[None], (GROUPS, 8, OBS_DP * HID)), DP)
    columns, sent = pl.pallas_call(
        product_kernel,
        out_shape=(
            jax.ShapeDtypeStruct((OBS, ORDER), f32),
            jax.ShapeDtypeStruct((GROUPS, OBS + 8, ROWS), f32),
        ),
        in_specs=[VMEM] * 3,
        out_specs=(VMEM, VMEM),
    )(gathered, covariance, predicted)
    products = exchanged(sent, DP)
    grams = pl.pallas_call(
        gram_kernel,
        out_shape=jax.ShapeDtypeStruct((8, OBS // 2, LANES), f32),
        in_specs=[VMEM] * 2,
        out_specs=VMEM,
    )(columns, products)
    near = pl.pallas_call(
        summed_kernel,
        out_shape=jax.ShapeDtypeStruct((4, OBS // 2, LANES), f32),
        in_specs=[VMEM],
        out_specs=VMEM,
    )(exchanged(grams, ("block_1", "block_2")))
    return pl.pallas_call(
        update_kernel,
        out_shape=(
            jax.ShapeDtypeStruct((1, ROWS), f32),
            jax.ShapeDtypeStruct((1, ROWS, ORDER), f32),
        ),
        in_specs=[SMEM] + [VMEM] * 6,
        out_specs=(VMEM, VMEM),
        scratch_shapes=[pltpu.VMEM((OBS, ORDER), f32)],
    )(
        place,
        exchanged(near, "block_0"),
        products,
        covariance,
        window,
        targets[None],
        noise_level[None],
    )


def solution(mesh):
    finer = Mesh(
        mesh.devices.reshape(4, 4, 4, 4, 2), ("dp_0", "dp_1", "block_0", "block_1", "block_2")
    )
    placed = (
        P(None, DP_BLOCK),
        P(None, DP_BLOCK),
        P(DP_BLOCK),
        P(DP_BLOCK),
        P(DP_BLOCK),
        P(),
        P(),
        P(),
        P(),
        P(),
        P(),
        P(),
        P(),
        P(),
        P(BLOCK, DP, None),
    )
    weighting = OBS / (LOCAL_STRUCTS * mesh.devices.size)
    return jax.shard_map(
        functools.partial(local, weighting=weighting),
        mesh=finer,
        in_specs=placed,
        out_specs=(P(BLOCK, DP), P(BLOCK, DP, None)),
        check_vma=False,
    )
```

time: 415 us -> 141 us (0.34); the launches traced: 410 us -> 141 us
  local copies, waits for them, and re-layouts: 129 us -> 0.04 us
  other arithmetic: 76.8 us -> 1.72 us
  matrix products: 29.2 us -> 0 us
  blocking collectives: 128 us -> 102 us
  Pallas kernels: 0 us -> 25.6 us
  waiting for transfers between devices: 26.1 us -> 1.73 us
  starting transfers between devices: 19.4 us -> 8.73 us
    all_to_all x0 -> x6, blocking collectives: none -> 102 us  [exchanged(): return lax.all_to_all(tiles, axes, split_axis=0, concat_axis=0, tiled=True)]
    gather x8 -> x0, local copies, waits for them, and re-layouts: 102 us -> none  [the longest x5 75.7 us: site_energy(): displace = coords[:, neighbour_at] - coords[:, None, :]]
    psum x5 -> x0, blocking collectives: 83.4 us -> none  [by_axis(): return functools.reduce(lax.psum, axes, array)]
    all_gather x4 -> x0, blocking collectives: 44.6 us -> none  [gather_in_order(): tiles = lax.all_gather(tiles, axes[k], axis=0, tiled=True)]
    dot_general x28 -> x0, matrix products: 28.9 us -> none  [the longest x14 14.4 us: site_energy(): jnp.dot(middle.T, first_layer, precision=highest) + middle_bias[:, None]]
    all_to_all x1 -> x0, waiting for transfers between devices: 26.1 us -> none  [summed_on_arrival(): lax.all_to_all(tiles, axis, split_axis=0, concat_axis=0, tiled=True)]
    reduce_sum x15 -> x2, other arithmetic: 26 us -> 0.04 us  [the longest x1 0.03 us: local(): across_y = jnp.sum(exchanged(partner, 'block_1'), axis=0)]
    scatter-add x5 -> x0, other arithmetic: 25.7 us -> none  [the longest x1 22.7 us: site_energy(): displace = coords[:, neighbour_at] - coords[:, None, :]]
  transfers between devices with their start and end apart: 1 -> 1, of which waited for: 1 -> 1; matrix products, arithmetic and copies ran while one was open for 6% -> 0% of each run, Pallas kernels for 0% -> 0%
where the time goes in v1:
time: 141 us
  blocking collectives  102 us (72%)
  Pallas kernels  25.6 us (18%)
  starting transfers between devices  8.73 us (6%)
  waiting for transfers between devices  1.73 us (1%)
  other arithmetic  1.72 us (1%)
    all_to_all x6, blocking collectives, exchanged(): return lax.all_to_all(tiles, axes, split_axis=0, concat_axis=0, tiled=True)  102 us
    pallas_call x1, Pallas kernels, local(): pl.pallas_call(update_kernel, out_shape=(jax.ShapeDtypeStruct((1, ROWS),...  9.95 us
    ppermute x1, starting transfers between devices, local(): partner = mine + lax.ppermute(theirs, 'block_2', [(0, 1), (1, 0)])  8.73 us
    pallas_call x1, Pallas kernels, local(): pl.pallas_call(functools.partial(jacobian_kernel, weighting=weighting), o...  7.8 us
    pallas_call x1, Pallas kernels, local(): pl.pallas_call(product_kernel, out_shape=(jax.ShapeDtypeStruct((OBS, ORDE...  3.45 us
    pallas_call x1, Pallas kernels, local(): pl.pallas_call(gram_kernel, out_shape=jax.ShapeDtypeStruct((8, OBS // 2,...  2.89 us
  transfers between devices with their start and end apart: 1, of which 1 were waited for; matrix products, arithmetic and copies ran while one was open for 0% of the time, Pallas kernels for 0%

profile of v1, /device:TPU:1, one launch (start us, length us, event | category | flops | bytes accessed | tf_op | source)
XLA Modules:
  0.0 140.6 jit_solution(15639270222384930123)
XLA Ops:
  0.6 0.6 pad_add_fusion.place
  1.2 7.8 %shard_map.158 = (f32[4,4,8,1024]{3,2,1,0:T(8,128)}, f32[4,4,8,1024]{3,2,1,0:T(8,128)}, f32[8,128]{1,0:T(8,128)}, f32[1,128]{1,0:T(1,128)}) custom-call(s32[3]{0:T(128)} %pad_add_fusion.place, s32[8]{0:T(128)} %tagged.1, s32[8]{0:T(128)} %observed.1, f32[3,256]{1,0:T(4,128)} %positions.1, s32[16,256]{1,0:T(8,128)} %neighbours.1, s32[1,256]{1,0:T(1,128)} %bitcast.8, ...), custom_call_target="tpu_custom_call" | custom-call | tf_op jit(solution)/shard_map/pallas_call | solution.py:293
  9.0 8.7 %collective-permute-start = (f32[4,4,8,1024]{3,2,1,0:T(8,128)}, f32[4,4,8,1024]{3,2,1,0:T(8,128)S(1)}, u32[]{:S(2)}, u32[]{:S(2)}) collective-permute-start(f32[4,4,8,1024]{3,2,1,0:T(8,128)} %get-tuple-element.9), channel_id=1, source_target_pairs={{0,1},{1,0},{2,3},{3,2},{4,5},{5,4},{6,7},{7,6},{8,9},{9,8},{10,11... | collective-permute-start | bytes 1572872 | tf_op jit(solution)/shard_map/ppermute | solution.py:325
  17.7 1.7 %collective-permute-done = f32[4,4,8,1024]{3,2,1,0:T(8,128)S(1)} collective-permute-done((f32[4,4,8,1024]{3,2,1,0:T(8,128)}, f32[4,4,8,1024]{3,2,1,0:T(8,128)S(1)}, u32[]{:S(2)}, u32[]{:S(2)}) %collective-permute-start) | collective-permute-done | bytes 524320 | tf_op jit(solution)/shard_map/ppermute | solution.py:325
  19.5 1.1 add.15
  20.6 11.6 %all_to_all.30 = f32[4,4,8,1024]{3,2,1,0:T(8,128)S(1)} all-to-all(f32[4,4,8,1024]{3,2,1,0:T(8,128)S(1)} %add.15), channel_id=1, replica_groups=mesh['dp_0'=4,'dp_1'=4,'block_0'=4,'block_1'=4,'block_2'=2] {'block_1'}, dimensions={0} | all-to-all | bytes 1048576 | tf_op jit(solution)/shard_map/all_to_all | solution.py:268
  32.2 22.5 %all_to_all.31 = f32[4,8,1024]{2,1,0:T(8,128)S(1)} all-to-all(f32[4,8,1024]{2,1,0:T(8,128)S(1)} %reduce_sum.18), channel_id=1, replica_groups=mesh['dp_0'=4,'dp_1'=4,'block_0'=4,'block_1'=4,'block_2'=2] {'block_0'}, dimensions={0} | all-to-all | bytes 262144 | tf_op jit(solution)/shard_map/all_to_all | solution.py:268
  54.8 17.0 %all_to_all.32.gathered = f32[16,8,1024]{2,1,0:T(8,128)} all-to-all(f32[16,8,1024]{2,1,0:T(8,128)S(1)} %broadcast_in_dim.24), channel_id=1, replica_groups=mesh['dp_0'=4,'dp_1'=4,'block_0'=4,'block_1'=4,'block_2'=2] {'dp_0','dp_1'}, dimensions={0} | all-to-all | bytes 1048576 | tf_op jit(solution)/shard_map/all_to_all | solution.py:268
  71.7 3.4 %shard_map.159 = (f32[64,2048]{1,0:T(8,128)}, f32[16,72,128]{2,1,0:T(8,128)}) custom-call(f32[16,8,1024]{2,1,0:T(8,128)} %all_to_all.32.gathered, f32[1,128,2048]{2,1,0:T(8,128)} %covariance.3, f32[8,128]{1,0:T(8,128)} %get-tuple-element.10.predicted), custom_call_target="tpu_custom_call" | custom-call | tf_op jit(solution)/shard_map/pallas_call | solution.py:329
  75.2 22.8 %all_to_all.33.products = f32[16,72,128]{2,1,0:T(8,128)} all-to-all(f32[16,72,128]{2,1,0:T(8,128)} %get-tuple-element.12), channel_id=1, replica_groups=mesh['dp_0'=4,'dp_1'=4,'block_0'=4,'block_1'=4,'block_2'=2] {'dp_0','dp_1'}, dimensions={0} | all-to-all | bytes 1179648 | tf_op jit(solution)/shard_map/all_to_all | solution.py:268
  98.0 2.9 %shard_map.160 = f32[8,32,128]{2,1,0:T(8,128)} custom-call(f32[64,2048]{1,0:T(8,128)} %get-tuple-element.11.columns, f32[16,72,128]{2,1,0:T(8,128)} %all_to_all.33.products), custom_call_target="tpu_custom_call" | custom-call | tf_op jit(solution)/shard_map/pallas_call | solution.py:339
  100.9 11.6 %all_to_all.34.arrived = f32[8,32,128]{2,1,0:T(8,128)} all-to-all(f32[8,32,128]{2,1,0:T(8,128)} %shard_map.160), channel_id=1, replica_groups=mesh['dp_0'=4,'dp_1'=4,'block_0'=4,'block_1'=4,'block_2'=2] {'block_1','..., dimensions={0} | all-to-all | bytes 262144 | tf_op jit(solution)/shard_map/all_to_all | solution.py:268
  112.5 1.5 %shard_map.161 = f32[4,32,128]{2,1,0:T(8,128)} custom-call(f32[8,32,128]{2,1,0:T(8,128)} %all_to_all.34.arrived), custom_call_target="tpu_custom_call" | custom-call | tf_op jit(solution)/shard_map/pallas_call | solution.py:345
  114.0 16.7 %all_to_all.35.arrived = f32[4,32,128]{2,1,0:T(8,128)} all-to-all(f32[4,32,128]{2,1,0:T(8,128)} %shard_map.161), channel_id=1, replica_groups=mesh['dp_0'=4,'dp_1'=4,'block_0'=4,'block_1'=4,'block_2'=2] {'block_0'}, dimensions={0} | all-to-all | bytes 131072 | tf_op jit(solution)/shard_map/all_to_all | solution.py:268
  130.7 9.9 %shard_map.162 = (f32[1,128]{1,0:T(1,128)}, f32[1,128,2048]{2,1,0:T(8,128)}) custom-call(s32[3]{0:T(128)} %pad_add_fusion.place, f32[4,32,128]{2,1,0:T(8,128)} %all_to_all.35.arrived, f32[16,72,128]{2,1,0:T(8,128)} %all_to_all.33.products, f32[1,128,2048]{2,1,0:T(8,128)} %covariance.3, f32[1,128]{1,0:T(1,128)} %get-tuple-element.13.window, ...), custom_call_target="tpu_custom_call" | custom-call | tf_op jit(solution)/shard_map/pallas_call | solution.py:351
  (3 shorter events, 0.1 us)
Async XLA Ops:
  9.0 10.5 %collective-permute-start = (f32[4,4,8,1024]{3,2,1,0:T(8,128)}, f32[4,4,8,1024]{3,2,1,0:T(8,128)S(1)}, u32[]{:S(2)}, u32[]{:S(2)}) collective-permute-start(f32[4,4,8,1024]{3,2,1,0:T(8,128)} %get-tuple-element.9), channel_id=1, source_target_pairs={{0,1},{1,0},{2,3},{3,2},{4,5},{5,4},{6,7},{7,6},{8,9},{9,8},{10,11... | collective-permute-start | bytes 1572872 | tf_op jit(solution)/shard_map/ppermute | solution.py:325

commit v2 on v1

--- a/solution.py
+++ b/solution.py
@@ -30,12 +30,22 @@
 
 VMEM = pl.BlockSpec(memory_space=pltpu.VMEM)
 SMEM = pl.BlockSpec(memory_space=pltpu.SMEM)
+HBM = pl.BlockSpec(memory_space=pltpu.HBM)
+
+
+def granted(mib):
+    return pltpu.CompilerParams(vmem_limit_bytes=mib * 1024 * 1024)
 
 
 def contract(lhs, rhs, over):
     return lax.dot_general(
         lhs, rhs, ((over[:1], over[1:]), ((), ())), precision=highest, preferred_element_type=jnp.float32
     )
+
+
+def halves(values):
+    upper = values.astype(jnp.bfloat16)
+    return upper, (values - upper.astype(jnp.float32)).astype(jnp.bfloat16)
 
 
 def along_lanes(row, at):
@@ -53,23 +63,33 @@
     species,
     scale,
     shift,
-    first_weight,
+    first_source,
     first_bias,
-    middle_weight,
+    middle_source,
     middle_bias,
     energy_weight,
+    targets,
+    noise,
     mine,
     theirs,
     predicted,
-    window,
+    kept,
     tables,
     descriptor,
     forward,
+    features,
     heads,
     jacobian,
+    first_weight,
+    middle_weight,
+    arrivals,
     weighting,
 ):
     core, block, group = place[0], place[1], place[2]
+    first_copy = pltpu.make_async_copy(first_source, first_weight, arrivals.at[0])
+    middle_copy = pltpu.make_async_copy(middle_source, middle_weight, arrivals.at[1])
+    first_copy.start()
+    middle_copy.start()
     for kind, table in enumerate((scale, shift)):
         columns = table[:].T
         for s in range(4):
@@ -131,10 +151,15 @@
 
         lax.fori_loop(0, EMB // 16, embed, 0)
 
+    first_copy.wait()
     inner = contract(descriptor[:], first_weight[:], (0, 0))
     first = jnp.tanh(inner[:ATOMS] + first_bias[:])
     forward[:ATOMS] = first
     forward[ATOMS:] = (1.0 - first * first) * inner[ATOMS:]
+    upper, lower = halves(forward[:])
+    features[: 2 * ATOMS] = upper
+    features[2 * ATOMS :] = lower
+    middle_copy.wait()
     outer = contract(forward[:], middle_weight[:], (1, 0))
     second = jnp.tanh(outer[:ATOMS] + middle_bias[:])
     bend = 1.0 - second * second
@@ -150,8 +175,10 @@
         rows = slice(s * STRUCT, (s + 1) * STRUCT)
         q = observed[s]
         is_energy = q == 0
-        direct = jnp.where(is_energy, slope[rows] * (weighting / STRUCT), slope_dot[rows] * -weighting)
-        through = slope[rows] * -weighting
+        direct = halves(
+            jnp.where(is_energy, slope[rows] * (weighting / STRUCT), slope_dot[rows] * -weighting)
+        )
+        through = halves(slope[rows] * -weighting)
         value = jnp.sum(
             jnp.where(is_energy, energy[rows] * (weighting / STRUCT), force[rows] * weighting),
             axis=0,
@@ -159,24 +186,35 @@
         )
         for o in range(OBS_DP):
             columns = slice(o * HID, (o + 1) * HID)
-            heads[s * STRUCT : (s + 1) * STRUCT, columns] = jnp.where(q == o, direct, 0.0)
-            heads[ATOMS + s * STRUCT : ATOMS + (s + 1) * STRUCT, columns] = jnp.where(
-                q == o, through, 0.0
-            )
+            for kind, pair in enumerate((direct, through)):
+                for part in range(2):
+                    start = (1 - part) * 2 * ATOMS + kind * ATOMS + s * STRUCT
+                    heads[start : start + STRUCT, columns] = jnp.where(
+                        q == o, pair[part], jnp.bfloat16(0)
+                    )
             sums[o] = sums[o] + jnp.where(q == o, value, 0.0)
     predicted[:] = jnp.zeros((8, LANES), jnp.float32)
     for o in range(OBS_DP):
         predicted[o : o + 1, :] = sums[o][:, :LANES] + sums[o][:, LANES:]
-    jacobian[:] = contract(forward[:], heads[:], (0, 0))
+    jacobian[:] = lax.dot_general(
+        features[:], heads[:], (((0,), (0,)), ((), ())), preferred_element_type=jnp.float32
+    ) + lax.dot_general(
+        features[: 2 * ATOMS],
+        heads[2 * ATOMS :],
+        (((0,), (0,)), ((), ())),
+        preferred_element_type=jnp.float32,
+    )
     for y in range(4):
         for z in range(4):
             pair = (z * 8 + y * 2) * 8
-            kept = pl.multiple_of(pair + core * 8, 8)
-            sent = pl.multiple_of(pair + (1 - core) * 8, 8)
-            mine[y, z] = jacobian[pl.ds(kept, 8), :]
-            theirs[y, z] = jacobian[pl.ds(sent, 8), :]
+            ours = pl.multiple_of(pair + core * 8, 8)
+            other = pl.multiple_of(pair + (1 - core) * 8, 8)
+            mine[y, z] = jacobian[pl.ds(ours, 8), :]
+            theirs[y, z] = jacobian[pl.ds(other, 8), :]
     line = middle_weight[pl.ds(block * 8 + group // 2, 1), :]
-    window[:] = jnp.where(group % 2 == 0, line[:, :LANES], line[:, LANES:])
+    kept[0:1] = jnp.where(group % 2 == 0, line[:, :LANES], line[:, LANES:])
+    kept[1:2] = jnp.concatenate([targets[:], noise[:]], axis=1)
+    kept[2:8] = jnp.zeros((6, LANES), jnp.float32)
 
 
 def product_kernel(gathered, covariance, predicted, columns, sent):
@@ -224,7 +262,16 @@
 
 
 def update_kernel(
-    place, arrived, products, covariance, window, targets, noise, new_weights, new_covariance, wide
+    place,
+    arrived,
+    products,
+    covariance,
+    kept,
+    new_weights,
+    new_covariance,
+    wide,
+    result,
+    departures,
 ):
     group = place[2]
     half = OBS // 2
@@ -242,26 +289,54 @@
     down = lax.broadcasted_iota(jnp.int32, (OBS, OBS), 0)
     across = lax.broadcasted_iota(jnp.int32, (OBS, OBS), 1)
     source = across == down % GROUPS * OBS_DP + down // GROUPS
-    noise_here = jnp.sum(jnp.where(source, noise[:], 0.0), axis=1, keepdims=True)
-    target_here = jnp.sum(jnp.where(source, targets[:], 0.0), axis=1, keepdims=True)
+    noise_here = jnp.sum(jnp.where(source, kept[1:2, OBS:], 0.0), axis=1, keepdims=True)
+    target_here = jnp.sum(jnp.where(source, kept[1:2, :OBS], 0.0), axis=1, keepdims=True)
     identity = (down == across).astype(jnp.float32)
     gram = gram + jnp.where(down == across, noise_here, 0.0)
     work = jnp.concatenate([gram, identity], axis=1)
-    below = lax.broadcasted_iota(jnp.int32, (OBS, 1), 0)
-    pivots = jnp.ones((OBS, 1), jnp.float32)
-    for k in range(OBS):
-        row = work[k : k + 1, :]
-        pivot = row[:, k : k + 1]
-        factor = jnp.where(below > k, work[:, k : k + 1] / pivot, 0.0)
-        pivots = jnp.where(below == k, pivot, pivots)
-        work = work - factor * row
-    root = work[:, OBS:] * lax.rsqrt(pivots)
+    strips = [work[8 * k : 8 * k + 8] for k in range(8)]
+    sublane = lax.broadcasted_iota(jnp.int32, (8, LANES), 0)
+    roots = []
+    for k in range(8):
+        active = range(k, 8)
+        panel = [
+            {r: jnp.broadcast_to(strips[r][:, 8 * k + j : 8 * k + j + 1], (8, LANES)) for r in active}
+            for j in range(8)
+        ]
+        pivots = jnp.ones((8, LANES), jnp.float32)
+        for j in range(8):
+            pivot = jnp.broadcast_to(panel[j][k][j : j + 1], (8, LANES))
+            pivots = jnp.where(sublane == j, pivot, pivots)
+            inverse = 1.0 / pivot
+            factor = {r: panel[j][r] * inverse for r in active}
+            factor[k] = jnp.where(sublane > j, factor[k], 0.0)
+            for n in range(j + 1, 8):
+                head = jnp.broadcast_to(panel[n][k][j : j + 1], (8, LANES))
+                for r in active:
+                    panel[n][r] = panel[n][r] - factor[r] * head
+            row = jnp.broadcast_to(strips[k][j : j + 1], (8, LANES))
+            for r in active:
+                strips[r] = strips[r] - factor[r] * row
+        roots.append(strips[k] * lax.rsqrt(pivots))
+    root = jnp.concatenate(roots, axis=0)[:, OBS:]
     for d in range(GROUPS):
         wide[:, d * ROWS : (d + 1) * ROWS] = products[d, :OBS]
     own = products[group, :OBS]
     gain = contract(root, contract(root, own, (1, 0)), (0, 0))
-    new_weights[:] = window[:] + jnp.sum(gain * (target_here - observed), axis=0, keepdims=True)
-    new_covariance[0] = (covariance[0] - contract(gain, wide[:], (0, 0))) / forgetting
+    new_weights[:] = kept[0:1] + jnp.sum(gain * (target_here - observed), axis=0, keepdims=True)
+    turned = gain.T
+    copies = []
+    for c in range(4):
+        columns = slice(c * ORDER // 4, (c + 1) * ORDER // 4)
+        update = contract(turned, wide[:, columns], (1, 0))
+        result[:, columns] = (covariance[0, :, columns] - update) / forgetting
+        copy = pltpu.make_async_copy(
+            result.at[:, columns], new_covariance.at[0, :, columns], departures.at[c]
+        )
+        copy.start()
+        copies.append(copy)
+    for copy in copies:
+        copy.wait()
 
 
 def exchanged(tiles, axes):
@@ -290,23 +365,28 @@
     place = jnp.stack(
         [lax.axis_index("block_2"), lax.axis_index(BLOCK), lax.axis_index(DP)]
     ).astype(jnp.int32)
-    mine, theirs, predicted, window = pl.pallas_call(
+    mine, theirs, predicted, kept = pl.pallas_call(
         functools.partial(jacobian_kernel, weighting=weighting),
         out_shape=(
             jax.ShapeDtypeStruct((4, 4, 8, OBS_DP * HID), f32),
             jax.ShapeDtypeStruct((4, 4, 8, OBS_DP * HID), f32),
             jax.ShapeDtypeStruct((8, LANES), f32),
-            jax.ShapeDtypeStruct((1, LANES), f32),
+            jax.ShapeDtypeStruct((8, LANES), f32),
         ),
-        in_specs=[SMEM, SMEM, SMEM] + [VMEM] * 10,
+        in_specs=[SMEM] * 3 + [VMEM] * 5 + [HBM, VMEM, HBM] + [VMEM] * 4,
         out_specs=(VMEM, VMEM, VMEM, VMEM),
         scratch_shapes=[
             pltpu.VMEM((8, EMB, LANES), f32),
             pltpu.VMEM((EMB, 2 * ATOMS), f32),
             pltpu.VMEM((2 * ATOMS, HID), f32),
-            pltpu.VMEM((2 * ATOMS, OBS_DP * HID), f32),
+            pltpu.VMEM((4 * ATOMS, HID), jnp.bfloat16),
+            pltpu.VMEM((4 * ATOMS, OBS_DP * HID), jnp.bfloat16),
             pltpu.VMEM((HID, OBS_DP * HID), f32),
+            pltpu.VMEM((EMB, HID), f32),
+            pltpu.VMEM((HID, HID), f32),
+            pltpu.SemaphoreType.DMA((2,)),
         ],
+        compiler_params=granted(12),
     )(
         place,
         tagged_atom,
@@ -316,11 +396,13 @@
         atom_species[None],
         embed_scale,
         embed_shift,
-        first_weight,
+        pltpu.with_memory_space_constraint(first_weight, pltpu.HBM),
         first_bias[None],
-        middle_weight,
+        pltpu.with_memory_space_constraint(middle_weight, pltpu.HBM),
         middle_bias[None],
         energy_weight,
+        targets[None],
+        noise_level[None],
     )
     partner = mine + lax.ppermute(theirs, "block_2", [(0, 1), (1, 0)])
     across_y = jnp.sum(exchanged(partner, "block_1"), axis=0)
@@ -334,6 +416,7 @@
         ),
         in_specs=[VMEM] * 3,
         out_specs=(VMEM, VMEM),
+        compiler_params=granted(8),
     )(gathered, covariance, predicted)
     products = exchanged(sent, DP)
     grams = pl.pallas_call(
@@ -341,12 +424,14 @@
         out_shape=jax.ShapeDtypeStruct((8, OBS // 2, LANES), f32),
         in_specs=[VMEM] * 2,
         out_specs=VMEM,
+        compiler_params=granted(8),
     )(columns, products)
     near = pl.pallas_call(
         summed_kernel,
         out_shape=jax.ShapeDtypeStruct((4, OBS // 2, LANES), f32),
         in_specs=[VMEM],
         out_specs=VMEM,
+        compiler_params=granted(4),
     )(exchanged(grams, ("block_1", "block_2")))
     return pl.pallas_call(
         update_kernel,
@@ -354,17 +439,20 @@
             jax.ShapeDtypeStruct((1, ROWS), f32),
             jax.ShapeDtypeStruct((1, ROWS, ORDER), f32),
         ),
-        in_specs=[SMEM] + [VMEM] * 6,
-        out_specs=(VMEM, VMEM),
-        scratch_shapes=[pltpu.VMEM((OBS, ORDER), f32)],
+        in_specs=[SMEM] + [VMEM] * 4,
+        out_specs=(VMEM, HBM),
+        scratch_shapes=[
+            pltpu.VMEM((OBS, ORDER), f32),
+            pltpu.VMEM((ROWS, ORDER), f32),
+            pltpu.SemaphoreType.DMA((4,)),
+        ],
+        compiler_params=granted(12),
     )(
         place,
         exchanged(near, "block_0"),
         products,
         covariance,
-        window,
-        targets[None],
-        noise_level[None],
+        kept,
     )
 
 

time: 141 us -> 126 us (0.89)
  Pallas kernels: 25.6 us -> 13.5 us
  blocking collectives: 102 us -> 100 us
  other arithmetic: 1.72 us -> 0.17 us
    pallas_call x1, Pallas kernels: 9.95 us -> 5.3 us  [local(): pl.pallas_call(update_kernel, out_shape=(jax.ShapeDtypeStruct((1, ROWS),...]
    pallas_call x1, Pallas kernels: 3.45 us -> 1.33 us  [local(): pl.pallas_call(product_kernel, out_shape=(jax.ShapeDtypeStruct((OBS, ORDE...]
    pallas_call x1, Pallas kernels: 7.8 us -> 5.88 us  [local(): pl.pallas_call(functools.partial(jacobian_kernel, weighting=weighting), o...]
    pallas_call x1, Pallas kernels: 2.89 us -> 1.02 us  [local(): pl.pallas_call(gram_kernel, out_shape=jax.ShapeDtypeStruct((8, OBS // 2,...]
    all_to_all x6, blocking collectives: 102 us -> 100 us  [exchanged(): return lax.all_to_all(tiles, axes, split_axis=0, concat_axis=0, tiled=True)]
    pallas_call x1, Pallas kernels: 1.55 us -> 0.01 us  [local(): pl.pallas_call(summed_kernel, out_shape=jax.ShapeDtypeStruct((4, OBS // 2...]
where the time goes in v2:
time: 126 us
  blocking collectives  100 us (79%)
  Pallas kernels  13.5 us (11%)
  starting transfers between devices  8.74 us (7%)
  waiting for transfers between devices  1.51 us (1%)
    all_to_all x6, blocking collectives, exchanged(): return lax.all_to_all(tiles, axes, split_axis=0, concat_axis=0, tiled=True)  100 us
    ppermute x1, starting transfers between devices, local(): partner = mine + lax.ppermute(theirs, 'block_2', [(0, 1), (1, 0)])  8.74 us
    pallas_call x1, Pallas kernels, local(): pl.pallas_call(functools.partial(jacobian_kernel, weighting=weighting), o...  5.88 us
    pallas_call x1, Pallas kernels, local(): pl.pallas_call(update_kernel, out_shape=(jax.ShapeDtypeStruct((1, ROWS),...  5.3 us
  transfers between devices with their start and end apart: 1, of which 1 were waited for; matrix products, arithmetic and copies ran while one was open for 0% of the time, Pallas kernels for 0%

profile of v2, /device:TPU:1, one launch (start us, length us, event | category | flops | bytes accessed | tf_op | source)
XLA Modules:
  0.0 126.0 jit_solution(9488202265525894706)
XLA Ops:
  0.7 0.1 pad_add_fusion.place
  0.8 0.5 copy-done.11
  1.3 0.0 copy-done.12
  1.3 0.1 copy-done.1
  1.4 0.0 copy-done.8
  1.4 0.0 copy-done.5
  1.4 0.0 copy-done.4
  1.5 0.1 copy-done.3
  1.5 0.0 copy-done.2
  1.5 0.0 copy-done.6
  1.5 5.9 %shard_map.158 = (f32[4,4,8,1024]{3,2,1,0:T(8,128)S(1)}, f32[4,4,8,1024]{3,2,1,0:T(8,128)S(1)}, f32[8,128]{1,0:T(8,128)S(1)}, f32[8,128]{1,0:T(8,128)S(1)}) custom-call(s32[3]{0:T(128)S(1)} %pad_add_fusion.place, s32[8]{0:T(128)S(1)} %copy-done.9, s32[8]{0:T(128)S(1)} %copy-done.10, f32[3,256]{1,0:T(4,128)S(1)} %copy-done.2, s32[16,256]{1,0:T(8,128)S(1)} %copy-done.1, ...), custom_call_target="tpu_custom_call" | custom-call | tf_op jit(solution)/shard_map/pallas_call | solution.py:368
  7.4 8.7 %collective-permute-start = (f32[4,4,8,1024]{3,2,1,0:T(8,128)S(1)}, f32[4,4,8,1024]{3,2,1,0:T(8,128)S(1)}, u32[]{:S(2)}, u32[]{:S(2)}) collective-permute-start(f32[4,4,8,1024]{3,2,1,0:T(8,128)S(1)} %get-tuple-element.9), channel_id=1, source_target_pairs={{0,1},{1,0},{2,3},{3,2},{4,5},{5,4},{6,7},{7,6},{8,9},{9,8},{10,11... | collective-permute-start | bytes 1572872 | tf_op jit(solution)/shard_map/ppermute | solution.py:407
  16.2 1.5 %collective-permute-done = f32[4,4,8,1024]{3,2,1,0:T(8,128)S(1)} collective-permute-done((f32[4,4,8,1024]{3,2,1,0:T(8,128)S(1)}, f32[4,4,8,1024]{3,2,1,0:T(8,128)S(1)}, u32[]{:S(2)}, u32[]{:S(2)}) %collective-permute-start) | collective-permute-done | bytes 524320 | tf_op jit(solution)/shard_map/ppermute | solution.py:407
  17.7 0.1 add.15
  17.7 11.6 %all_to_all.30 = f32[4,4,8,1024]{3,2,1,0:T(8,128)S(1)} all-to-all(f32[4,4,8,1024]{3,2,1,0:T(8,128)S(1)} %add.15), channel_id=1, replica_groups=mesh['dp_0'=4,'dp_1'=4,'block_0'=4,'block_1'=4,'block_2'=2] {'block_1'}, dimensions={0} | all-to-all | bytes 1048576 | tf_op jit(solution)/shard_map/all_to_all | solution.py:343
  29.4 0.0 copy-start
  29.4 22.6 %all_to_all.31 = f32[4,8,1024]{2,1,0:T(8,128)S(1)} all-to-all(f32[4,8,1024]{2,1,0:T(8,128)S(1)} %reduce_sum.18), channel_id=1, replica_groups=mesh['dp_0'=4,'dp_1'=4,'block_0'=4,'block_1'=4,'block_2'=2] {'block_0'}, dimensions={0} | all-to-all | bytes 262144 | tf_op jit(solution)/shard_map/all_to_all | solution.py:343
  52.1 16.8 %all_to_all.32.gathered = f32[16,8,1024]{2,1,0:T(8,128)S(1)} all-to-all(f32[16,8,1024]{2,1,0:T(8,128)S(1)} %broadcast_in_dim.26), channel_id=1, replica_groups=mesh['dp_0'=4,'dp_1'=4,'block_0'=4,'block_1'=4,'block_2'=2] {'dp_0','dp_1'}, dimensions={0} | all-to-all | bytes 1048576 | tf_op jit(solution)/shard_map/all_to_all | solution.py:343
  68.8 1.3 %shard_map.159 = (f32[64,2048]{1,0:T(8,128)S(1)}, f32[16,72,128]{2,1,0:T(8,128)S(1)}) custom-call(f32[16,8,1024]{2,1,0:T(8,128)S(1)} %all_to_all.32.gathered, f32[1,128,2048]{2,1,0:T(8,128)S(1)} %copy-done, f32[8,128]{1,0:T(8,128)S(1)} %get-tuple-element.10.predicted), custom_call_target="tpu_custom_call" | custom-call | tf_op jit(solution)/shard_map/pallas_call | solution.py:411
  70.2 22.3 %all_to_all.33.products = f32[16,72,128]{2,1,0:T(8,128)S(1)} all-to-all(f32[16,72,128]{2,1,0:T(8,128)S(1)} %get-tuple-element.12), channel_id=1, replica_groups=mesh['dp_0'=4,'dp_1'=4,'block_0'=4,'block_1'=4,'block_2'=2] {'dp_0','dp_1'}, dimensions={0} | all-to-all | bytes 1179648 | tf_op jit(solution)/shard_map/all_to_all | solution.py:343
  92.5 1.0 shard_map.160
  93.5 10.0 %all_to_all.34.arrived = f32[8,32,128]{2,1,0:T(8,128)S(1)} all-to-all(f32[8,32,128]{2,1,0:T(8,128)S(1)} %shard_map.160), channel_id=1, replica_groups=mesh['dp_0'=4,'dp_1'=4,'block_0'=4,'block_1'=4,'block_2'=2] {'block_1','..., dimensions={0} | all-to-all | bytes 262144 | tf_op jit(solution)/shard_map/all_to_all | solution.py:343
  103.5 17.1 %all_to_all.35.arrived = f32[4,32,128]{2,1,0:T(8,128)S(1)} all-to-all(f32[4,32,128]{2,1,0:T(8,128)S(1)} %shard_map.161), channel_id=1, replica_groups=mesh['dp_0'=4,'dp_1'=4,'block_0'=4,'block_1'=4,'block_2'=2] {'block_0'}, dimensions={0} | all-to-all | bytes 131072 | tf_op jit(solution)/shard_map/all_to_all | solution.py:343
  120.7 5.3 %shard_map.162 = (f32[1,128]{1,0:T(1,128)}, f32[1,128,2048]{2,1,0:T(8,128)}) custom-call(s32[3]{0:T(128)S(1)} %pad_add_fusion.place, f32[4,32,128]{2,1,0:T(8,128)S(1)} %all_to_all.35.arrived, f32[16,72,128]{2,1,0:T(8,128)S(1)} %all_to_all.33.products, f32[1,128,2048]{2,1,0:T(8,128)S(1)} %copy-done, f32[8,128]{1,0:T(8,128)S(1)} %get-tuple-element.13.kept), custom_call_target="tpu_custom_call" | custom-call | tf_op jit(solution)/shard_map/pallas_call | solution.py:436
  (20 shorter events, 0.1 us)
Async XLA Ops:
  0.6 0.7 copy-start.11
  0.7 0.7 copy-start.12
  0.7 0.7 copy-start.1
  0.7 0.7 copy-start.9
  0.7 0.7 copy-start.10
  0.7 0.7 copy-start.7
  0.7 0.7 copy-start.8
  0.7 0.7 copy-start.5
  0.7 0.7 copy-start.4
  0.8 0.7 copy-start.3
  0.8 0.7 copy-start.2
  0.8 0.7 copy-start.6
  7.4 10.3 %collective-permute-start = (f32[4,4,8,1024]{3,2,1,0:T(8,128)S(1)}, f32[4,4,8,1024]{3,2,1,0:T(8,128)S(1)}, u32[]{:S(2)}, u32[]{:S(2)}) collective-permute-start(f32[4,4,8,1024]{3,2,1,0:T(8,128)S(1)} %get-tuple-element.9), channel_id=1, source_target_pairs={{0,1},{1,0},{2,3},{3,2},{4,5},{5,4},{6,7},{7,6},{8,9},{9,8},{10,11... | collective-permute-start | bytes 1572872 | tf_op jit(solution)/shard_map/ppermute | solution.py:407
  29.4 39.5 %copy-start = (f32[1,128,2048]{2,1,0:T(8,128)S(1)}, f32[1,128,2048]{2,1,0:T(8,128)}, u32[]{:S(2)}) copy-start(f32[1,128,2048]{2,1,0:T(8,128)} %covariance.3) | copy-start | bytes 3145732

commit v3 on v2

--- a/solution.py
+++ b/solution.py
@@ -46,6 +46,17 @@
 def halves(values):
     upper = values.astype(jnp.bfloat16)
     return upper, (values - upper.astype(jnp.float32)).astype(jnp.bfloat16)
+
+
+def stacked(values, order):
+    pair = halves(values)
+    return jnp.concatenate([pair[n] for n in order], axis=0)
+
+
+def plain(lhs, rhs, over):
+    return lax.dot_general(
+        lhs, rhs, ((over[:1], over[1:]), ((), ())), preferred_element_type=jnp.float32
+    )
 
 
 def along_lanes(row, at):
@@ -76,9 +87,7 @@
     kept,
     tables,
     descriptor,
-    forward,
     features,
-    heads,
     jacobian,
     first_weight,
     middle_weight,
@@ -152,15 +161,23 @@
         lax.fori_loop(0, EMB // 16, embed, 0)
 
     first_copy.wait()
-    inner = contract(descriptor[:], first_weight[:], (0, 0))
+    inner = plain(
+        stacked(descriptor[:], (0, 1, 0)), stacked(first_weight[:], (0, 0, 1)), (0, 0)
+    )
     first = jnp.tanh(inner[:ATOMS] + first_bias[:])
-    forward[:ATOMS] = first
-    forward[ATOMS:] = (1.0 - first * first) * inner[ATOMS:]
-    upper, lower = halves(forward[:])
-    features[: 2 * ATOMS] = upper
-    features[2 * ATOMS :] = lower
+    upper, lower = halves(
+        jnp.concatenate([first, (1.0 - first * first) * inner[ATOMS:]], axis=0)
+    )
+    for s in range(LOCAL_STRUCTS):
+        for n, piece in enumerate((upper, upper, lower, lower)):
+            source = n % 2 * ATOMS + s * STRUCT
+            start = (s * 4 + n) * STRUCT
+            features[start : start + STRUCT] = piece[source : source + STRUCT]
     middle_copy.wait()
-    outer = contract(forward[:], middle_weight[:], (1, 0))
+    wide, narrow = halves(middle_weight[:])
+    outer = (plain(upper, narrow, (1, 0)) + plain(lower, wide, (1, 0))) + plain(
+        upper, wide, (1, 0)
+    )
     second = jnp.tanh(outer[:ATOMS] + middle_bias[:])
     bend = 1.0 - second * second
     second_dot = bend * outer[ATOMS:]
@@ -170,47 +187,49 @@
     slope_dot = -2.0 * readout * second * second_dot
     energy = readout * second
     force = -(readout * second_dot)
+    turned = features[:].T
+    jacobian[:] = jnp.zeros((OBS_DP, HID, HID), jnp.float32)
     sums = [jnp.zeros((1, HID), jnp.float32) for _ in range(OBS_DP)]
     for s in range(LOCAL_STRUCTS):
         rows = slice(s * STRUCT, (s + 1) * STRUCT)
         q = observed[s]
         is_energy = q == 0
-        direct = halves(
-            jnp.where(is_energy, slope[rows] * (weighting / STRUCT), slope_dot[rows] * -weighting)
+        head, tail = halves(
+            jnp.concatenate(
+                [
+                    jnp.where(
+                        is_energy, slope[rows] * (weighting / STRUCT), slope_dot[rows] * -weighting
+                    ),
+                    slope[rows] * -weighting,
+                ],
+                axis=0,
+            )
         )
-        through = halves(slope[rows] * -weighting)
         value = jnp.sum(
             jnp.where(is_energy, energy[rows] * (weighting / STRUCT), force[rows] * weighting),
             axis=0,
             keepdims=True,
         )
         for o in range(OBS_DP):
-            columns = slice(o * HID, (o + 1) * HID)
-            for kind, pair in enumerate((direct, through)):
-                for part in range(2):
-                    start = (1 - part) * 2 * ATOMS + kind * ATOMS + s * STRUCT
-                    heads[start : start + STRUCT, columns] = jnp.where(
-                        q == o, pair[part], jnp.bfloat16(0)
-                    )
             sums[o] = sums[o] + jnp.where(q == o, value, 0.0)
+        lanes = turned[:, s * 4 * STRUCT : (s + 1) * 4 * STRUCT]
+        jacobian[q] += plain(
+            jnp.concatenate([lanes, lanes], axis=1),
+            jnp.concatenate([head, head, tail, jnp.zeros_like(tail)], axis=0),
+            (1, 0),
+        )
     predicted[:] = jnp.zeros((8, LANES), jnp.float32)
     for o in range(OBS_DP):
         predicted[o : o + 1, :] = sums[o][:, :LANES] + sums[o][:, LANES:]
-    jacobian[:] = lax.dot_general(
-        features[:], heads[:], (((0,), (0,)), ((), ())), preferred_element_type=jnp.float32
-    ) + lax.dot_general(
-        features[: 2 * ATOMS],
-        heads[2 * ATOMS :],
-        (((0,), (0,)), ((), ())),
-        preferred_element_type=jnp.float32,
-    )
     for y in range(4):
         for z in range(4):
             pair = (z * 8 + y * 2) * 8
             ours = pl.multiple_of(pair + core * 8, 8)
             other = pl.multiple_of(pair + (1 - core) * 8, 8)
-            mine[y, z] = jacobian[pl.ds(ours, 8), :]
-            theirs[y, z] = jacobian[pl.ds(other, 8), :]
+            for q in range(OBS_DP):
+                columns = slice(q * HID, (q + 1) * HID)
+                mine[y, z, :, columns] = jacobian[q, pl.ds(ours, 8), :]
+                theirs[y, z, :, columns] = jacobian[q, pl.ds(other, 8), :]
     line = middle_weight[pl.ds(block * 8 + group // 2, 1), :]
     kept[0:1] = jnp.where(group % 2 == 0, line[:, :LANES], line[:, LANES:])
     kept[1:2] = jnp.concatenate([targets[:], noise[:]], axis=1)
@@ -304,31 +323,42 @@
             for j in range(8)
         ]
         pivots = jnp.ones((8, LANES), jnp.float32)
-        for j in range(8):
-            pivot = jnp.broadcast_to(panel[j][k][j : j + 1], (8, LANES))
-            pivots = jnp.where(sublane == j, pivot, pivots)
-            inverse = 1.0 / pivot
-            factor = {r: panel[j][r] * inverse for r in active}
-            factor[k] = jnp.where(sublane > j, factor[k], 0.0)
-            for n in range(j + 1, 8):
+        for j in range(0, 8, 2):
+            left, right = panel[j], panel[j + 1]
+            top = jnp.broadcast_to(left[k][j : j + 1], (8, LANES))
+            side = jnp.broadcast_to(right[k][j : j + 1], (8, LANES))
+            corner = jnp.broadcast_to(right[k][j + 1 : j + 2], (8, LANES))
+            area = top * corner - side * side
+            inverse = 1.0 / area
+            one = {r: (left[r] * corner - right[r] * side) * inverse for r in active}
+            two = {r: (right[r] * top - left[r] * side) * inverse for r in active}
+            one[k] = jnp.where(sublane > j + 1, one[k], 0.0)
+            two[k] = jnp.where(sublane > j + 1, two[k], 0.0)
+            for n in range(j + 2, 8):
                 head = jnp.broadcast_to(panel[n][k][j : j + 1], (8, LANES))
+                tail = jnp.broadcast_to(panel[n][k][j + 1 : j + 2], (8, LANES))
                 for r in active:
-                    panel[n][r] = panel[n][r] - factor[r] * head
-            row = jnp.broadcast_to(strips[k][j : j + 1], (8, LANES))
+                    panel[n][r] = panel[n][r] - (one[r] * head + two[r] * tail)
+            head = jnp.broadcast_to(strips[k][j : j + 1], (8, LANES))
+            tail = jnp.broadcast_to(strips[k][j + 1 : j + 2], (8, LANES))
             for r in active:
-                strips[r] = strips[r] - factor[r] * row
+                strips[r] = strips[r] - (one[r] * head + two[r] * tail)
+            ratio = 1.0 / top
+            strips[k] = jnp.where(sublane == j + 1, strips[k] - side * ratio * head, strips[k])
+            pivots = jnp.where(sublane == j, top, pivots)
+            pivots = jnp.where(sublane == j + 1, area * ratio, pivots)
         roots.append(strips[k] * lax.rsqrt(pivots))
     root = jnp.concatenate(roots, axis=0)[:, OBS:]
     for d in range(GROUPS):
-        wide[:, d * ROWS : (d + 1) * ROWS] = products[d, :OBS]
+        wide[:, d * ROWS : (d + 1) * ROWS] = stacked(products[d, :OBS], (0, 0, 1))
     own = products[group, :OBS]
     gain = contract(root, contract(root, own, (1, 0)), (0, 0))
     new_weights[:] = kept[0:1] + jnp.sum(gain * (target_here - observed), axis=0, keepdims=True)
-    turned = gain.T
+    turned = stacked(gain, (0, 1, 0))
     copies = []
     for c in range(4):
         columns = slice(c * ORDER // 4, (c + 1) * ORDER // 4)
-        update = contract(turned, wide[:, columns], (1, 0))
+        update = plain(turned, wide[:, columns], (0, 0))
         result[:, columns] = (covariance[0, :, columns] - update) / forgetting
         copy = pltpu.make_async_copy(
             result.at[:, columns], new_covariance.at[0, :, columns], departures.at[c]
@@ -378,10 +408,8 @@
         scratch_shapes=[
             pltpu.VMEM((8, EMB, LANES), f32),
             pltpu.VMEM((EMB, 2 * ATOMS), f32),
-            pltpu.VMEM((2 * ATOMS, HID), f32),
             pltpu.VMEM((4 * ATOMS, HID), jnp.bfloat16),
-            pltpu.VMEM((4 * ATOMS, OBS_DP * HID), jnp.bfloat16),
-            pltpu.VMEM((HID, OBS_DP * HID), f32),
+            pltpu.VMEM((OBS_DP, HID, HID), f32),
             pltpu.VMEM((EMB, HID), f32),
             pltpu.VMEM((HID, HID), f32),
             pltpu.SemaphoreType.DMA((2,)),
@@ -442,7 +470,7 @@
         in_specs=[SMEM] + [VMEM] * 4,
         out_specs=(VMEM, HBM),
         scratch_shapes=[
-            pltpu.VMEM((OBS, ORDER), f32),
+            pltpu.VMEM((3 * OBS, ORDER), jnp.bfloat16),
             pltpu.VMEM((ROWS, ORDER), f32),
             pltpu.SemaphoreType.DMA((4,)),
         ],

time: 126 us -> 124 us (0.984)
  Pallas kernels: 13.5 us -> 11.4 us
    pallas_call x1, Pallas kernels: 5.88 us -> 4.25 us  [local(): pl.pallas_call(functools.partial(jacobian_kernel, weighting=weighting), o...]
where the time goes in v3:
time: 124 us; the launch traced here: 123 us
  blocking collectives  99.9 us (81%)
  Pallas kernels  11.4 us (9%)
  starting transfers between devices  8.75 us (7%)
  waiting for transfers between devices  1.51 us (1%)
    all_to_all x6, blocking collectives, exchanged(): return lax.all_to_all(tiles, axes, split_axis=0, concat_axis=0, tiled=True)  99.9 us
    ppermute x1, starting transfers between devices, local(): partner = mine + lax.ppermute(theirs, 'block_2', [(0, 1), (1, 0)])  8.75 us
    pallas_call x1, Pallas kernels, local(): pl.pallas_call(update_kernel, out_shape=(jax.ShapeDtypeStruct((1, ROWS),...  4.78 us
    pallas_call x1, Pallas kernels, local(): pl.pallas_call(functools.partial(jacobian_kernel, weighting=weighting), o...  4.25 us
  transfers between devices with their start and end apart: 1, of which 1 were waited for; matrix products, arithmetic and copies ran while one was open for 0% of the time, Pallas kernels for 0%

profile of v3, /device:TPU:1, one launch (start us, length us, event | category | flops | bytes accessed | tf_op | source)
XLA Modules:
  0.0 123.3 jit_solution(8571177502286851952)
XLA Ops:
  0.7 0.1 pad_add_fusion.place
  0.8 0.5 copy-done.11
  1.3 0.0 copy-done.12
  1.3 0.1 copy-done.1
  1.4 0.0 copy-done.8
  1.4 0.0 copy-done.5
  1.4 0.0 copy-done.4
  1.5 0.1 copy-done.3
  1.5 0.0 copy-done.2
  1.5 0.0 copy-done.6
  1.5 4.3 %shard_map.158 = (f32[4,4,8,1024]{3,2,1,0:T(8,128)S(1)}, f32[4,4,8,1024]{3,2,1,0:T(8,128)S(1)}, f32[8,128]{1,0:T(8,128)S(1)}, f32[8,128]{1,0:T(8,128)S(1)}) custom-call(s32[3]{0:T(128)S(1)} %pad_add_fusion.place, s32[8]{0:T(128)S(1)} %copy-done.9, s32[8]{0:T(128)S(1)} %copy-done.10, f32[3,256]{1,0:T(4,128)S(1)} %copy-done.2, s32[16,256]{1,0:T(8,128)S(1)} %copy-done.1, ...), custom_call_target="tpu_custom_call" | custom-call | tf_op jit(solution)/shard_map/pallas_call | solution.py:398
  5.8 8.7 %collective-permute-start = (f32[4,4,8,1024]{3,2,1,0:T(8,128)S(1)}, f32[4,4,8,1024]{3,2,1,0:T(8,128)S(1)}, u32[]{:S(2)}, u32[]{:S(2)}) collective-permute-start(f32[4,4,8,1024]{3,2,1,0:T(8,128)S(1)} %get-tuple-element.9), channel_id=1, source_target_pairs={{0,1},{1,0},{2,3},{3,2},{4,5},{5,4},{6,7},{7,6},{8,9},{9,8},{10,11... | collective-permute-start | bytes 1572872 | tf_op jit(solution)/shard_map/ppermute | solution.py:435
  14.5 1.5 %collective-permute-done = f32[4,4,8,1024]{3,2,1,0:T(8,128)S(1)} collective-permute-done((f32[4,4,8,1024]{3,2,1,0:T(8,128)S(1)}, f32[4,4,8,1024]{3,2,1,0:T(8,128)S(1)}, u32[]{:S(2)}, u32[]{:S(2)}) %collective-permute-start) | collective-permute-done | bytes 524320 | tf_op jit(solution)/shard_map/ppermute | solution.py:435
  16.1 0.1 add.15
  16.1 11.6 %all_to_all.30 = f32[4,4,8,1024]{3,2,1,0:T(8,128)S(1)} all-to-all(f32[4,4,8,1024]{3,2,1,0:T(8,128)S(1)} %add.15), channel_id=1, replica_groups=mesh['dp_0'=4,'dp_1'=4,'block_0'=4,'block_1'=4,'block_2'=2] {'block_1'}, dimensions={0} | all-to-all | bytes 1048576 | tf_op jit(solution)/shard_map/all_to_all | solution.py:373
  27.8 0.0 copy-start
  27.8 22.6 %all_to_all.31 = f32[4,8,1024]{2,1,0:T(8,128)S(1)} all-to-all(f32[4,8,1024]{2,1,0:T(8,128)S(1)} %reduce_sum.18), channel_id=1, replica_groups=mesh['dp_0'=4,'dp_1'=4,'block_0'=4,'block_1'=4,'block_2'=2] {'block_0'}, dimensions={0} | all-to-all | bytes 262144 | tf_op jit(solution)/shard_map/all_to_all | solution.py:373
  50.4 16.9 %all_to_all.32.gathered = f32[16,8,1024]{2,1,0:T(8,128)S(1)} all-to-all(f32[16,8,1024]{2,1,0:T(8,128)S(1)} %broadcast_in_dim.26), channel_id=1, replica_groups=mesh['dp_0'=4,'dp_1'=4,'block_0'=4,'block_1'=4,'block_2'=2] {'dp_0','dp_1'}, dimensions={0} | all-to-all | bytes 1048576 | tf_op jit(solution)/shard_map/all_to_all | solution.py:373
  67.3 1.3 %shard_map.159 = (f32[64,2048]{1,0:T(8,128)S(1)}, f32[16,72,128]{2,1,0:T(8,128)S(1)}) custom-call(f32[16,8,1024]{2,1,0:T(8,128)S(1)} %all_to_all.32.gathered, f32[1,128,2048]{2,1,0:T(8,128)S(1)} %copy-done, f32[8,128]{1,0:T(8,128)S(1)} %get-tuple-element.10.predicted), custom_call_target="tpu_custom_call" | custom-call | tf_op jit(solution)/shard_map/pallas_call | solution.py:439
  68.6 22.5 %all_to_all.33.products = f32[16,72,128]{2,1,0:T(8,128)S(1)} all-to-all(f32[16,72,128]{2,1,0:T(8,128)S(1)} %get-tuple-element.12), channel_id=1, replica_groups=mesh['dp_0'=4,'dp_1'=4,'block_0'=4,'block_1'=4,'block_2'=2] {'dp_0','dp_1'}, dimensions={0} | all-to-all | bytes 1179648 | tf_op jit(solution)/shard_map/all_to_all | solution.py:373
  91.1 1.0 shard_map.160
  92.1 10.0 %all_to_all.34.arrived = f32[8,32,128]{2,1,0:T(8,128)S(1)} all-to-all(f32[8,32,128]{2,1,0:T(8,128)S(1)} %shard_map.160), channel_id=1, replica_groups=mesh['dp_0'=4,'dp_1'=4,'block_0'=4,'block_1'=4,'block_2'=2] {'block_1','..., dimensions={0} | all-to-all | bytes 262144 | tf_op jit(solution)/shard_map/all_to_all | solution.py:373
  102.2 16.4 %all_to_all.35.arrived = f32[4,32,128]{2,1,0:T(8,128)S(1)} all-to-all(f32[4,32,128]{2,1,0:T(8,128)S(1)} %shard_map.161), channel_id=1, replica_groups=mesh['dp_0'=4,'dp_1'=4,'block_0'=4,'block_1'=4,'block_2'=2] {'block_0'}, dimensions={0} | all-to-all | bytes 131072 | tf_op jit(solution)/shard_map/all_to_all | solution.py:373
  118.6 4.8 %shard_map.162 = (f32[1,128]{1,0:T(1,128)}, f32[1,128,2048]{2,1,0:T(8,128)}) custom-call(s32[3]{0:T(128)S(1)} %pad_add_fusion.place, f32[4,32,128]{2,1,0:T(8,128)S(1)} %all_to_all.35.arrived, f32[16,72,128]{2,1,0:T(8,128)S(1)} %all_to_all.33.products, f32[1,128,2048]{2,1,0:T(8,128)S(1)} %copy-done, f32[8,128]{1,0:T(8,128)S(1)} %get-tuple-element.13.kept), custom_call_target="tpu_custom_call" | custom-call | tf_op jit(solution)/shard_map/pallas_call | solution.py:464
  (20 shorter events, 0.1 us)
Async XLA Ops:
  0.6 0.7 copy-start.11
  0.7 0.7 copy-start.12
  0.7 0.7 copy-start.1
  0.7 0.7 copy-start.9
  0.7 0.7 copy-start.10
  0.7 0.7 copy-start.7
  0.7 0.7 copy-start.8
  0.7 0.7 copy-start.5
  0.7 0.7 copy-start.4
  0.8 0.7 copy-start.3
  0.8 0.7 copy-start.2
  0.8 0.7 copy-start.6
  5.8 10.3 %collective-permute-start = (f32[4,4,8,1024]{3,2,1,0:T(8,128)S(1)}, f32[4,4,8,1024]{3,2,1,0:T(8,128)S(1)}, u32[]{:S(2)}, u32[]{:S(2)}) collective-permute-start(f32[4,4,8,1024]{3,2,1,0:T(8,128)S(1)} %get-tuple-element.9), channel_id=1, source_target_pairs={{0,1},{1,0},{2,3},{3,2},{4,5},{5,4},{6,7},{7,6},{8,9},{9,8},{10,11... | collective-permute-start | bytes 1572872 | tf_op jit(solution)/shard_map/ppermute | solution.py:435
  27.8 39.5 %copy-start = (f32[1,128,2048]{2,1,0:T(8,128)S(1)}, f32[1,128,2048]{2,1,0:T(8,128)}, u32[]{:S(2)}) copy-start(f32[1,128,2048]{2,1,0:T(8,128)} %covariance.3) | copy-start | bytes 3145732

commit v4 on v3

--- a/solution.py
+++ b/solution.py
@@ -66,9 +66,9 @@
 
 
 def jacobian_kernel(
-    place,
-    tagged,
-    observed,
+    tags,
+    parts,
+    observed_source,
     positions,
     neighbours,
     species,
@@ -91,10 +91,14 @@
     jacobian,
     first_weight,
     middle_weight,
+    observed,
     arrivals,
     weighting,
 ):
-    core, block, group = place[0], place[1], place[2]
+    core = lax.axis_index("block_2")
+    block, group = lax.axis_index(BLOCK), lax.axis_index(DP)
+    observed_copy = pltpu.make_async_copy(observed_source, observed, arrivals.at[2])
+    observed_copy.start()
     first_copy = pltpu.make_async_copy(first_source, first_weight, arrivals.at[0])
     middle_copy = pltpu.make_async_copy(middle_source, middle_weight, arrivals.at[1])
     first_copy.start()
@@ -110,8 +114,9 @@
         part = jnp.zeros((SLOTS, LANES), jnp.int32)
         for s in range(4):
             here = lane // STRUCT == s
-            tag = jnp.where(here, tagged[half * 4 + s], tag)
-            part = jnp.where(here, observed[half * 4 + s], part)
+            own = slice(half * 4 + s, half * 4 + s + 1)
+            tag = jnp.where(here, tags[:, own], tag)
+            part = jnp.where(here, parts[:, own], part)
         listed = neighbours[:, lanes]
         within = jnp.minimum(listed, STRUCT - 1)
         at = lane // STRUCT * STRUCT + within
@@ -188,6 +193,7 @@
     energy = readout * second
     force = -(readout * second_dot)
     turned = features[:].T
+    observed_copy.wait()
     jacobian[:] = jnp.zeros((OBS_DP, HID, HID), jnp.float32)
     sums = [jnp.zeros((1, HID), jnp.float32) for _ in range(OBS_DP)]
     for s in range(LOCAL_STRUCTS):
@@ -248,10 +254,10 @@
         sent[d, OBS:] = predicted[:]
 
 
-def gram_kernel(columns, products, sent):
-    gram = jnp.zeros((OBS, OBS), jnp.float32)
+def gram_kernel(columns, products, sent, wide):
     for d in range(GROUPS):
-        gram = gram + contract(columns[:, d * ROWS : (d + 1) * ROWS], products[d, :OBS], (1, 1))
+        wide[:, d * ROWS : (d + 1) * ROWS] = products[d, :OBS]
+    gram = contract(columns[:], wide[:], (1, 1))
     half = OBS // 2
     values = jnp.sum(
         jnp.concatenate([products[:, OBS + q, :] for q in range(OBS_DP)], axis=0),
@@ -281,9 +287,9 @@
 
 
 def update_kernel(
-    place,
     arrived,
     products,
+    sent,
     covariance,
     kept,
     new_weights,
@@ -292,14 +298,14 @@
     result,
     departures,
 ):
-    group = place[2]
     half = OBS // 2
     packed = (arrived[0] + arrived[1]) + (arrived[2] + arrived[3])
-    corner = packed[:, half:OBS]
     gram = jnp.concatenate(
         [
-            packed[:, :OBS],
-            jnp.concatenate([corner.T, packed[:, OBS : OBS + half]], axis=1),
+            jnp.concatenate([packed[:, :half], 2.0 * packed[:, half:OBS]], axis=1),
+            jnp.concatenate(
+                [jnp.zeros((half, half), jnp.float32), packed[:, OBS : OBS + half]], axis=1
+            ),
         ],
         axis=0,
     )
@@ -316,42 +322,45 @@
     strips = [work[8 * k : 8 * k + 8] for k in range(8)]
     sublane = lax.broadcasted_iota(jnp.int32, (8, LANES), 0)
     roots = []
-    for k in range(8):
+    for k in range(0, 8, 2):
         active = range(k, 8)
         panel = [
             {r: jnp.broadcast_to(strips[r][:, 8 * k + j : 8 * k + j + 1], (8, LANES)) for r in active}
-            for j in range(8)
+            for j in range(16)
         ]
-        pivots = jnp.ones((8, LANES), jnp.float32)
-        for j in range(0, 8, 2):
+        pivots = {k: jnp.ones((8, LANES), jnp.float32), k + 1: jnp.ones((8, LANES), jnp.float32)}
+        for j in range(0, 16, 2):
+            c, i = k + j // 8, j % 8
             left, right = panel[j], panel[j + 1]
-            top = jnp.broadcast_to(left[k][j : j + 1], (8, LANES))
-            side = jnp.broadcast_to(right[k][j : j + 1], (8, LANES))
-            corner = jnp.broadcast_to(right[k][j + 1 : j + 2], (8, LANES))
+            live = range(c, 8)
+            top = jnp.broadcast_to(left[c][i : i + 1], (8, LANES))
+            side = jnp.broadcast_to(right[c][i : i + 1], (8, LANES))
+            corner = jnp.broadcast_to(right[c][i + 1 : i + 2], (8, LANES))
             area = top * corner - side * side
             inverse = 1.0 / area
-            one = {r: (left[r] * corner - right[r] * side) * inverse for r in active}
-            two = {r: (right[r] * top - left[r] * side) * inverse for r in active}
-            one[k] = jnp.where(sublane > j + 1, one[k], 0.0)
-            two[k] = jnp.where(sublane > j + 1, two[k], 0.0)
-            for n in range(j + 2, 8):
-                head = jnp.broadcast_to(panel[n][k][j : j + 1], (8, LANES))
-                tail = jnp.broadcast_to(panel[n][k][j + 1 : j + 2], (8, LANES))
-                for r in active:
+            one = {r: (left[r] * corner - right[r] * side) * inverse for r in live}
+            two = {r: (right[r] * top - left[r] * side) * inverse for r in live}
+            one[c] = jnp.where(sublane > i + 1, one[c], 0.0)
+            two[c] = jnp.where(sublane > i + 1, two[c], 0.0)
+            for n in range(j + 2, 16):
+                head = jnp.broadcast_to(panel[n][c][i : i + 1], (8, LANES))
+                tail = jnp.broadcast_to(panel[n][c][i + 1 : i + 2], (8, LANES))
+                for r in live:
                     panel[n][r] = panel[n][r] - (one[r] * head + two[r] * tail)
-            head = jnp.broadcast_to(strips[k][j : j + 1], (8, LANES))
-            tail = jnp.broadcast_to(strips[k][j + 1 : j + 2], (8, LANES))
-            for r in active:
+            head = jnp.broadcast_to(strips[c][i : i + 1], (8, LANES))
+            tail = jnp.broadcast_to(strips[c][i + 1 : i + 2], (8, LANES))
+            for r in live:
                 strips[r] = strips[r] - (one[r] * head + two[r] * tail)
             ratio = 1.0 / top
-            strips[k] = jnp.where(sublane == j + 1, strips[k] - side * ratio * head, strips[k])
-            pivots = jnp.where(sublane == j, top, pivots)
-            pivots = jnp.where(sublane == j + 1, area * ratio, pivots)
-        roots.append(strips[k] * lax.rsqrt(pivots))
+            strips[c] = jnp.where(sublane == i + 1, strips[c] - side * ratio * head, strips[c])
+            pivots[c] = jnp.where(sublane == i, top, pivots[c])
+            pivots[c] = jnp.where(sublane == i + 1, area * ratio, pivots[c])
+        for c in (k, k + 1):
+            roots.append(strips[c] * lax.rsqrt(pivots[c]))
     root = jnp.concatenate(roots, axis=0)[:, OBS:]
     for d in range(GROUPS):
         wide[:, d * ROWS : (d + 1) * ROWS] = stacked(products[d, :OBS], (0, 0, 1))
-    own = products[group, :OBS]
+    own = sent[0, :OBS]
     gain = contract(root, contract(root, own, (1, 0)), (0, 0))
     new_weights[:] = kept[0:1] + jnp.sum(gain * (target_here - observed), axis=0, keepdims=True)
     turned = stacked(gain, (0, 1, 0))
@@ -392,9 +401,6 @@
     weighting,
 ):
     f32 = jnp.float32
-    place = jnp.stack(
-        [lax.axis_index("block_2"), lax.axis_index(BLOCK), lax.axis_index(DP)]
-    ).astype(jnp.int32)
     mine, theirs, predicted, kept = pl.pallas_call(
         functools.partial(jacobian_kernel, weighting=weighting),
         out_shape=(
@@ -403,7 +409,7 @@
             jax.ShapeDtypeStruct((8, LANES), f32),
             jax.ShapeDtypeStruct((8, LANES), f32),
         ),
-        in_specs=[SMEM] * 3 + [VMEM] * 5 + [HBM, VMEM, HBM] + [VMEM] * 4,
+        in_specs=[VMEM, VMEM, HBM] + [VMEM] * 5 + [HBM, VMEM, HBM] + [VMEM] * 4,
         out_specs=(VMEM, VMEM, VMEM, VMEM),
         scratch_shapes=[
             pltpu.VMEM((8, EMB, LANES), f32),
@@ -412,25 +418,31 @@
             pltpu.VMEM((OBS_DP, HID, HID), f32),
             pltpu.VMEM((EMB, HID), f32),
             pltpu.VMEM((HID, HID), f32),
-            pltpu.SemaphoreType.DMA((2,)),
+            pltpu.SMEM((LOCAL_STRUCTS,), jnp.int32),
+            pltpu.SemaphoreType.DMA((3,)),
         ],
         compiler_params=granted(12),
     )(
-        place,
-        tagged_atom,
-        observed_in,
-        positions,
-        neighbours,
-        atom_species[None],
-        embed_scale,
-        embed_shift,
-        pltpu.with_memory_space_constraint(first_weight, pltpu.HBM),
-        first_bias[None],
-        pltpu.with_memory_space_constraint(middle_weight, pltpu.HBM),
-        middle_bias[None],
-        energy_weight,
-        targets[None],
-        noise_level[None],
+        *(
+            pltpu.with_memory_space_constraint(operand, pltpu.HBM)
+            for operand in (
+                tagged_atom[None],
+                observed_in[None],
+                observed_in,
+                positions,
+                neighbours,
+                atom_species[None],
+                embed_scale,
+                embed_shift,
+                first_weight,
+                first_bias[None],
+                middle_weight,
+                middle_bias[None],
+                energy_weight,
+                targets[None],
+                noise_level[None],
+            )
+        )
     )
     partner = mine + lax.ppermute(theirs, "block_2", [(0, 1), (1, 0)])
     across_y = jnp.sum(exchanged(partner, "block_1"), axis=0)
@@ -452,6 +464,7 @@
         out_shape=jax.ShapeDtypeStruct((8, OBS // 2, LANES), f32),
         in_specs=[VMEM] * 2,
         out_specs=VMEM,
+        scratch_shapes=[pltpu.VMEM((OBS, ORDER), f32)],
         compiler_params=granted(8),
     )(columns, products)
     near = pl.pallas_call(
@@ -467,7 +480,7 @@
             jax.ShapeDtypeStruct((1, ROWS), f32),
             jax.ShapeDtypeStruct((1, ROWS, ORDER), f32),
         ),
-        in_specs=[SMEM] + [VMEM] * 4,
+        in_specs=[VMEM] * 5,
         out_specs=(VMEM, HBM),
         scratch_shapes=[
             pltpu.VMEM((3 * OBS, ORDER), jnp.bfloat16),
@@ -476,9 +489,9 @@
         ],
         compiler_params=granted(12),
     )(
-        place,
         exchanged(near, "block_0"),
         products,
+        sent,
         covariance,
         kept,
     )

time: 124 us -> 122 us (0.984)
  no operation moved by 1% of the time
where the time goes in v4:
time: 122 us; the launch traced here: 121 us
  blocking collectives  100 us (82%)
  Pallas kernels  10.4 us (9%)
  starting transfers between devices  8.75 us (7%)
  waiting for transfers between devices  1.51 us (1%)
    all_to_all x6, blocking collectives, exchanged(): return lax.all_to_all(tiles, axes, split_axis=0, concat_axis=0, tiled=True)  100 us
    ppermute x1, starting transfers between devices, local(): partner = mine + lax.ppermute(theirs, 'block_2', [(0, 1), (1, 0)])  8.75 us
    pallas_call x1, Pallas kernels, local(): pl.pallas_call(functools.partial(jacobian_kernel, weighting=weighting), o...  4.57 us
    pallas_call x1, Pallas kernels, local(): pl.pallas_call(update_kernel, out_shape=(jax.ShapeDtypeStruct((1, ROWS),...  3.86 us
  transfers between devices with their start and end apart: 1, of which 1 were waited for; matrix products, arithmetic and copies ran while one was open for 0% of the time, Pallas kernels for 0%

profile of v4, /device:TPU:1, one launch (start us, length us, event | category | flops | bytes accessed | tf_op | source)
XLA Modules:
  0.0 121.5 jit_solution(12779218770653431315)
XLA Ops:
  0.6 4.6 %shard_map.158 = (f32[4,4,8,1024]{3,2,1,0:T(8,128)S(1)}, f32[4,4,8,1024]{3,2,1,0:T(8,128)S(1)}, f32[8,128]{1,0:T(8,128)S(1)}, f32[8,128]{1,0:T(8,128)S(1)}) custom-call(s32[1,8]{1,0:T(1,128)} %bitcast.11, s32[1,8]{1,0:T(1,128)} %bitcast.7, s32[8]{0:T(128)} %observed_source.1, f32[3,256]{1,0:T(4,128)} %positions.1, s32[16,256]{1,0:T(8,128)} %neighbours.1, ...), custom_call_target="tpu_custom_call" | custom-call | tf_op jit(solution)/shard_map/pallas_call | solution.py:404
  5.2 8.7 %collective-permute-start = (f32[4,4,8,1024]{3,2,1,0:T(8,128)S(1)}, f32[4,4,8,1024]{3,2,1,0:T(8,128)S(1)}, u32[]{:S(2)}, u32[]{:S(2)}) collective-permute-start(f32[4,4,8,1024]{3,2,1,0:T(8,128)S(1)} %get-tuple-element.9), channel_id=1, source_target_pairs={{0,1},{1,0},{2,3},{3,2},{4,5},{5,4},{6,7},{7,6},{8,9},{9,8},{10,11... | collective-permute-start | bytes 1572872 | tf_op jit(solution)/shard_map/ppermute | solution.py:447
  14.0 1.5 %collective-permute-done = f32[4,4,8,1024]{3,2,1,0:T(8,128)S(1)} collective-permute-done((f32[4,4,8,1024]{3,2,1,0:T(8,128)S(1)}, f32[4,4,8,1024]{3,2,1,0:T(8,128)S(1)}, u32[]{:S(2)}, u32[]{:S(2)}) %collective-permute-start) | collective-permute-done | bytes 524320 | tf_op jit(solution)/shard_map/ppermute | solution.py:447
  15.5 0.1 add.3
  15.5 11.6 %all_to_all.30 = f32[4,4,8,1024]{3,2,1,0:T(8,128)S(1)} all-to-all(f32[4,4,8,1024]{3,2,1,0:T(8,128)S(1)} %add.3), channel_id=1, replica_groups=mesh['dp_0'=4,'dp_1'=4,'block_0'=4,'block_1'=4,'block_2'=2] {'block_1'}, dimensions={0} | all-to-all | bytes 1048576 | tf_op jit(solution)/shard_map/all_to_all | solution.py:382
  27.2 0.0 copy-start
  27.2 22.6 %all_to_all.31 = f32[4,8,1024]{2,1,0:T(8,128)S(1)} all-to-all(f32[4,8,1024]{2,1,0:T(8,128)S(1)} %reduce_sum.18), channel_id=1, replica_groups=mesh['dp_0'=4,'dp_1'=4,'block_0'=4,'block_1'=4,'block_2'=2] {'block_0'}, dimensions={0} | all-to-all | bytes 262144 | tf_op jit(solution)/shard_map/all_to_all | solution.py:382
  49.9 16.9 %all_to_all.32.gathered = f32[16,8,1024]{2,1,0:T(8,128)S(1)} all-to-all(f32[16,8,1024]{2,1,0:T(8,128)S(1)} %broadcast_in_dim.34), channel_id=1, replica_groups=mesh['dp_0'=4,'dp_1'=4,'block_0'=4,'block_1'=4,'block_2'=2] {'dp_0','dp_1'}, dimensions={0} | all-to-all | bytes 1048576 | tf_op jit(solution)/shard_map/all_to_all | solution.py:382
  66.7 0.0 copy-done
  66.7 1.3 %shard_map.159 = (f32[64,2048]{1,0:T(8,128)S(1)}, f32[16,72,128]{2,1,0:T(8,128)S(1)}) custom-call(f32[16,8,1024]{2,1,0:T(8,128)S(1)} %all_to_all.32.gathered, f32[1,128,2048]{2,1,0:T(8,128)S(1)} %copy-done, f32[8,128]{1,0:T(8,128)S(1)} %get-tuple-element.10.predicted), custom_call_target="tpu_custom_call" | custom-call | tf_op jit(solution)/shard_map/pallas_call | solution.py:451
  68.1 22.5 %all_to_all.33.products = f32[16,72,128]{2,1,0:T(8,128)S(1)} all-to-all(f32[16,72,128]{2,1,0:T(8,128)S(1)} %get-tuple-element.12.sent), channel_id=1, replica_groups=mesh['dp_0'=4,'dp_1'=4,'block_0'=4,'block_1'=4,'block_2'=2] {'dp_0','dp_1'}, dimensions={0} | all-to-all | bytes 1179648 | tf_op jit(solution)/shard_map/all_to_all | solution.py:382
  90.6 0.6 shard_map.160
  91.2 10.0 %all_to_all.34.arrived = f32[8,32,128]{2,1,0:T(8,128)S(1)} all-to-all(f32[8,32,128]{2,1,0:T(8,128)S(1)} %shard_map.160), channel_id=1, replica_groups=mesh['dp_0'=4,'dp_1'=4,'block_0'=4,'block_1'=4,'block_2'=2] {'block_1','..., dimensions={0} | all-to-all | bytes 262144 | tf_op jit(solution)/shard_map/all_to_all | solution.py:382
  101.3 16.4 %all_to_all.35.arrived = f32[4,32,128]{2,1,0:T(8,128)S(1)} all-to-all(f32[4,32,128]{2,1,0:T(8,128)S(1)} %shard_map.161), channel_id=1, replica_groups=mesh['dp_0'=4,'dp_1'=4,'block_0'=4,'block_1'=4,'block_2'=2] {'block_0'}, dimensions={0} | all-to-all | bytes 131072 | tf_op jit(solution)/shard_map/all_to_all | solution.py:382
  117.6 3.9 %shard_map.162 = (f32[1,128]{1,0:T(1,128)}, f32[1,128,2048]{2,1,0:T(8,128)}) custom-call(f32[4,32,128]{2,1,0:T(8,128)S(1)} %all_to_all.35.arrived, f32[16,72,128]{2,1,0:T(8,128)S(1)} %all_to_all.33.products, f32[16,72,128]{2,1,0:T(8,128)S(1)} %get-tuple-element.12.sent, f32[1,128,2048]{2,1,0:T(8,128)S(1)} %copy-done, f32[8,128]{1,0:T(8,128)S(1)} %get-tuple-element.13.kept), custom_call_target="tpu_custom_call" | custom-call | tf_op jit(solution)/shard_map/pallas_call | solution.py:477
  (4 shorter events, 0.1 us)
Async XLA Ops:
  5.2 10.3 %collective-permute-start = (f32[4,4,8,1024]{3,2,1,0:T(8,128)S(1)}, f32[4,4,8,1024]{3,2,1,0:T(8,128)S(1)}, u32[]{:S(2)}, u32[]{:S(2)}) collective-permute-start(f32[4,4,8,1024]{3,2,1,0:T(8,128)S(1)} %get-tuple-element.9), channel_id=1, source_target_pairs={{0,1},{1,0},{2,3},{3,2},{4,5},{5,4},{6,7},{7,6},{8,9},{9,8},{10,11... | collective-permute-start | bytes 1572872 | tf_op jit(solution)/shard_map/ppermute | solution.py:447
  27.2 39.5 %copy-start = (f32[1,128,2048]{2,1,0:T(8,128)S(1)}, f32[1,128,2048]{2,1,0:T(8,128)}, u32[]{:S(2)}) copy-start(f32[1,128,2048]{2,1,0:T(8,128)} %covariance.3) | copy-start | bytes 3145732

commit v5 on v4

--- a/solution.py
+++ b/solution.py
@@ -245,9 +245,11 @@
 def product_kernel(gathered, covariance, predicted, columns, sent):
     for i in range(8):
         for q in range(OBS_DP):
-            columns[q * GROUPS : (q + 1) * GROUPS, i * HID : (i + 1) * HID] = gathered[
-                :, i, q * HID : (q + 1) * HID
-            ]
+            for z in range(4):
+                start = q * GROUPS + z * 4
+                columns[start : start + 4, i * HID : (i + 1) * HID] = gathered[
+                    :, z, i, q * HID : (q + 1) * HID
+                ]
     product = contract(columns[:], covariance[0], (1, 1))
     for d in range(GROUPS):
         sent[d, :OBS] = product
@@ -447,7 +449,8 @@
     partner = mine + lax.ppermute(theirs, "block_2", [(0, 1), (1, 0)])
     across_y = jnp.sum(exchanged(partner, "block_1"), axis=0)
     across_z = jnp.sum(exchanged(across_y, "block_0"), axis=0)
-    gathered = exchanged(jnp.broadcast_to(across_z[None], (GROUPS, 8, OBS_DP * HID)), DP)
+    along_z = exchanged(jnp.broadcast_to(across_z[None], (4, 8, OBS_DP * HID)), "dp_0")
+    gathered = exchanged(jnp.broadcast_to(along_z[None], (4, 4, 8, OBS_DP * HID)), "dp_1")
     columns, sent = pl.pallas_call(
         product_kernel,
         out_shape=(

time: 122 us -> 120 us (0.984)
  blocking collectives: 100 us -> 98.4 us
    all_to_all x6 -> x7, blocking collectives: 100 us -> 98.4 us  [exchanged(): return lax.all_to_all(tiles, axes, split_axis=0, concat_axis=0, tiled=True)]
where the time goes in v5:
time: 120 us
  blocking collectives  98.4 us (82%)
  Pallas kernels  10.5 us (9%)
  starting transfers between devices  8.75 us (7%)
  waiting for transfers between devices  1.51 us (1%)
    all_to_all x7, blocking collectives, exchanged(): return lax.all_to_all(tiles, axes, split_axis=0, concat_axis=0, tiled=True)  98.4 us
    ppermute x1, starting transfers between devices, local(): partner = mine + lax.ppermute(theirs, 'block_2', [(0, 1), (1, 0)])  8.75 us
    pallas_call x1, Pallas kernels, local(): pl.pallas_call(functools.partial(jacobian_kernel, weighting=weighting), o...  4.57 us
    pallas_call x1, Pallas kernels, local(): pl.pallas_call(update_kernel, out_shape=(jax.ShapeDtypeStruct((1, ROWS),...  3.86 us
  transfers between devices with their start and end apart: 1, of which 1 were waited for; matrix products, arithmetic and copies ran while one was open for 0% of the time, Pallas kernels for 0%

profile of v5, /device:TPU:1, one launch (start us, length us, event | category | flops | bytes accessed | tf_op | source)
XLA Modules:
  0.0 120.0 jit_solution(14763472567995168643)
XLA Ops:
  0.6 4.6 %shard_map.158 = (f32[4,4,8,1024]{3,2,1,0:T(8,128)S(1)}, f32[4,4,8,1024]{3,2,1,0:T(8,128)S(1)}, f32[8,128]{1,0:T(8,128)S(1)}, f32[8,128]{1,0:T(8,128)S(1)}) custom-call(s32[1,8]{1,0:T(1,128)} %bitcast.11, s32[1,8]{1,0:T(1,128)} %bitcast.7, s32[8]{0:T(128)} %observed_source.1, f32[3,256]{1,0:T(4,128)} %positions.1, s32[16,256]{1,0:T(8,128)} %neighbours.1, ...), custom_call_target="tpu_custom_call" | custom-call | tf_op jit(solution)/shard_map/pallas_call | solution.py:406
  5.2 8.7 %collective-permute-start = (f32[4,4,8,1024]{3,2,1,0:T(8,128)S(1)}, f32[4,4,8,1024]{3,2,1,0:T(8,128)S(1)}, u32[]{:S(2)}, u32[]{:S(2)}) collective-permute-start(f32[4,4,8,1024]{3,2,1,0:T(8,128)S(1)} %get-tuple-element.9), channel_id=1, source_target_pairs={{0,1},{1,0},{2,3},{3,2},{4,5},{5,4},{6,7},{7,6},{8,9},{9,8},{10,11... | collective-permute-start | bytes 1572872 | tf_op jit(solution)/shard_map/ppermute | solution.py:449
  14.0 1.5 %collective-permute-done = f32[4,4,8,1024]{3,2,1,0:T(8,128)S(1)} collective-permute-done((f32[4,4,8,1024]{3,2,1,0:T(8,128)S(1)}, f32[4,4,8,1024]{3,2,1,0:T(8,128)S(1)}, u32[]{:S(2)}, u32[]{:S(2)}) %collective-permute-start) | collective-permute-done | bytes 524320 | tf_op jit(solution)/shard_map/ppermute | solution.py:449
  15.5 0.1 add.3
  15.5 11.6 %all_to_all.35 = f32[4,4,8,1024]{3,2,1,0:T(8,128)S(1)} all-to-all(f32[4,4,8,1024]{3,2,1,0:T(8,128)S(1)} %add.3), channel_id=1, replica_groups=mesh['dp_0'=4,'dp_1'=4,'block_0'=4,'block_1'=4,'block_2'=2] {'block_1'}, dimensions={0} | all-to-all | bytes 1048576 | tf_op jit(solution)/shard_map/all_to_all | solution.py:384
  27.2 22.5 %all_to_all.36 = f32[4,8,1024]{2,1,0:T(8,128)S(1)} all-to-all(f32[4,8,1024]{2,1,0:T(8,128)S(1)} %reduce_sum.18), channel_id=1, replica_groups=mesh['dp_0'=4,'dp_1'=4,'block_0'=4,'block_1'=4,'block_2'=2] {'block_0'}, dimensions={0} | all-to-all | bytes 262144 | tf_op jit(solution)/shard_map/all_to_all | solution.py:384
  49.7 0.0 copy-start
  49.7 8.1 %all_to_all.37 = f32[4,8,1024]{2,1,0:T(8,128)S(1)} all-to-all(f32[4,8,1024]{2,1,0:T(8,128)S(1)} %broadcast_in_dim.40), channel_id=1, replica_groups=mesh['dp_0'=4,'dp_1'=4,'block_0'=4,'block_1'=4,'block_2'=2] {'dp_0'}, dimensions={0} | all-to-all | bytes 262144 | tf_op jit(solution)/shard_map/all_to_all | solution.py:384
  57.8 10.8 %all_to_all.38.gathered = f32[4,4,8,1024]{3,2,1,0:T(8,128)S(1)} all-to-all(f32[4,4,8,1024]{3,2,1,0:T(8,128)S(1)} %broadcast_in_dim.41), channel_id=1, replica_groups=mesh['dp_0'=4,'dp_1'=4,'block_0'=4,'block_1'=4,'block_2'=2] {'dp_1'}, dimensions={0} | all-to-all | bytes 1048576 | tf_op jit(solution)/shard_map/all_to_all | solution.py:384
  68.6 0.0 copy-done
  68.6 1.4 %shard_map.159 = (f32[64,2048]{1,0:T(8,128)S(1)}, f32[16,72,128]{2,1,0:T(8,128)S(1)}) custom-call(f32[4,4,8,1024]{3,2,1,0:T(8,128)S(1)} %all_to_all.38.gathered, f32[1,128,2048]{2,1,0:T(8,128)S(1)} %copy-done, f32[8,128]{1,0:T(8,128)S(1)} %get-tuple-element.10.predicted), custom_call_target="tpu_custom_call" | custom-call | tf_op jit(solution)/shard_map/pallas_call | solution.py:454
  69.9 15.2 %all_to_all.39.products = f32[16,72,128]{2,1,0:T(8,128)S(1)} all-to-all(f32[16,72,128]{2,1,0:T(8,128)S(1)} %get-tuple-element.12.sent), channel_id=1, replica_groups=mesh['dp_0'=4,'dp_1'=4,'block_0'=4,'block_1'=4,'block_2'=2] {'dp_0','dp_1'}, dimensions={0} | all-to-all | bytes 1179648 | tf_op jit(solution)/shard_map/all_to_all | solution.py:384
  85.1 0.7 shard_map.160
  85.8 15.7 %all_to_all.40.arrived = f32[8,32,128]{2,1,0:T(8,128)S(1)} all-to-all(f32[8,32,128]{2,1,0:T(8,128)S(1)} %shard_map.160), channel_id=1, replica_groups=mesh['dp_0'=4,'dp_1'=4,'block_0'=4,'block_1'=4,'block_2'=2] {'block_1','..., dimensions={0} | all-to-all | bytes 262144 | tf_op jit(solution)/shard_map/all_to_all | solution.py:384
  101.5 14.7 %all_to_all.41.arrived = f32[4,32,128]{2,1,0:T(8,128)S(1)} all-to-all(f32[4,32,128]{2,1,0:T(8,128)S(1)} %shard_map.161), channel_id=1, replica_groups=mesh['dp_0'=4,'dp_1'=4,'block_0'=4,'block_1'=4,'block_2'=2] {'block_0'}, dimensions={0} | all-to-all | bytes 131072 | tf_op jit(solution)/shard_map/all_to_all | solution.py:384
  116.1 3.9 %shard_map.162 = (f32[1,128]{1,0:T(1,128)}, f32[1,128,2048]{2,1,0:T(8,128)}) custom-call(f32[4,32,128]{2,1,0:T(8,128)S(1)} %all_to_all.41.arrived, f32[16,72,128]{2,1,0:T(8,128)S(1)} %all_to_all.39.products, f32[16,72,128]{2,1,0:T(8,128)S(1)} %get-tuple-element.12.sent, f32[1,128,2048]{2,1,0:T(8,128)S(1)} %copy-done, f32[8,128]{1,0:T(8,128)S(1)} %get-tuple-element.13.kept), custom_call_target="tpu_custom_call" | custom-call | tf_op jit(solution)/shard_map/pallas_call | solution.py:480
  (5 shorter events, 0.1 us)
Async XLA Ops:
  5.2 10.3 %collective-permute-start = (f32[4,4,8,1024]{3,2,1,0:T(8,128)S(1)}, f32[4,4,8,1024]{3,2,1,0:T(8,128)S(1)}, u32[]{:S(2)}, u32[]{:S(2)}) collective-permute-start(f32[4,4,8,1024]{3,2,1,0:T(8,128)S(1)} %get-tuple-element.9), channel_id=1, source_target_pairs={{0,1},{1,0},{2,3},{3,2},{4,5},{5,4},{6,7},{7,6},{8,9},{9,8},{10,11... | collective-permute-start | bytes 1572872 | tf_op jit(solution)/shard_map/ppermute | solution.py:449
  49.7 18.9 %copy-start = (f32[1,128,2048]{2,1,0:T(8,128)S(1)}, f32[1,128,2048]{2,1,0:T(8,128)}, u32[]{:S(2)}) copy-start(f32[1,128,2048]{2,1,0:T(8,128)} %covariance.3) | copy-start | bytes 3145732

commit v6 on v5

--- a/solution.py
+++ b/solution.py
@@ -187,7 +187,13 @@
     bend = 1.0 - second * second
     second_dot = bend * outer[ATOMS:]
     own = lax.broadcasted_iota(jnp.int32, (4, ATOMS), 0) == species[:]
-    readout = contract(own.astype(jnp.float32), energy_weight[:], (0, 0))
+    chosen_species = own.astype(jnp.float32).astype(jnp.bfloat16)
+    coarse, rest = energy_weight[:].astype(jnp.bfloat16), energy_weight[:]
+    rest = rest - coarse.astype(jnp.float32)
+    middle, fine = halves(rest)
+    readout = plain(chosen_species, coarse, (0, 0)) + (
+        plain(chosen_species, middle, (0, 0)) + plain(chosen_species, fine, (0, 0))
+    )
     slope = readout * bend
     slope_dot = -2.0 * readout * second * second_dot
     energy = readout * second

time: 120 us -> 120 us (level)
  no operation moved by 1% of the time
where the time goes in v6:
time: 120 us
  blocking collectives  98.4 us (82%)
  Pallas kernels  10.3 us (9%)
  starting transfers between devices  8.75 us (7%)
  waiting for transfers between devices  1.51 us (1%)
    all_to_all x7, blocking collectives, exchanged(): return lax.all_to_all(tiles, axes, split_axis=0, concat_axis=0, tiled=True)  98.4 us
    ppermute x1, starting transfers between devices, local(): partner = mine + lax.ppermute(theirs, 'block_2', [(0, 1), (1, 0)])  8.75 us
    pallas_call x1, Pallas kernels, local(): pl.pallas_call(functools.partial(jacobian_kernel, weighting=weighting), o...  4.42 us
    pallas_call x1, Pallas kernels, local(): pl.pallas_call(update_kernel, out_shape=(jax.ShapeDtypeStruct((1, ROWS),...  3.86 us
  transfers between devices with their start and end apart: 1, of which 1 were waited for; matrix products, arithmetic and copies ran while one was open for 0% of the time, Pallas kernels for 0%

profile of v6, /device:TPU:1, one launch (start us, length us, event | category | flops | bytes accessed | tf_op | source)
XLA Modules:
  0.0 119.8 jit_solution(9026990752025846828)
XLA Ops:
  0.6 4.4 %shard_map.158 = (f32[4,4,8,1024]{3,2,1,0:T(8,128)S(1)}, f32[4,4,8,1024]{3,2,1,0:T(8,128)S(1)}, f32[8,128]{1,0:T(8,128)S(1)}, f32[8,128]{1,0:T(8,128)S(1)}) custom-call(s32[1,8]{1,0:T(1,128)} %bitcast.11, s32[1,8]{1,0:T(1,128)} %bitcast.7, s32[8]{0:T(128)} %observed_source.1, f32[3,256]{1,0:T(4,128)} %positions.1, s32[16,256]{1,0:T(8,128)} %neighbours.1, ...), custom_call_target="tpu_custom_call" | custom-call | tf_op jit(solution)/shard_map/pallas_call | solution.py:412
  5.1 8.7 %collective-permute-start = (f32[4,4,8,1024]{3,2,1,0:T(8,128)S(1)}, f32[4,4,8,1024]{3,2,1,0:T(8,128)S(1)}, u32[]{:S(2)}, u32[]{:S(2)}) collective-permute-start(f32[4,4,8,1024]{3,2,1,0:T(8,128)S(1)} %get-tuple-element.9), channel_id=1, source_target_pairs={{0,1},{1,0},{2,3},{3,2},{4,5},{5,4},{6,7},{7,6},{8,9},{9,8},{10,11... | collective-permute-start | bytes 1572872 | tf_op jit(solution)/shard_map/ppermute | solution.py:455
  13.8 1.5 %collective-permute-done = f32[4,4,8,1024]{3,2,1,0:T(8,128)S(1)} collective-permute-done((f32[4,4,8,1024]{3,2,1,0:T(8,128)S(1)}, f32[4,4,8,1024]{3,2,1,0:T(8,128)S(1)}, u32[]{:S(2)}, u32[]{:S(2)}) %collective-permute-start) | collective-permute-done | bytes 524320 | tf_op jit(solution)/shard_map/ppermute | solution.py:455
  15.3 0.1 add.3
  15.4 11.6 %all_to_all.35 = f32[4,4,8,1024]{3,2,1,0:T(8,128)S(1)} all-to-all(f32[4,4,8,1024]{3,2,1,0:T(8,128)S(1)} %add.3), channel_id=1, replica_groups=mesh['dp_0'=4,'dp_1'=4,'block_0'=4,'block_1'=4,'block_2'=2] {'block_1'}, dimensions={0} | all-to-all | bytes 1048576 | tf_op jit(solution)/shard_map/all_to_all | solution.py:390
  27.0 22.5 %all_to_all.36 = f32[4,8,1024]{2,1,0:T(8,128)S(1)} all-to-all(f32[4,8,1024]{2,1,0:T(8,128)S(1)} %reduce_sum.18), channel_id=1, replica_groups=mesh['dp_0'=4,'dp_1'=4,'block_0'=4,'block_1'=4,'block_2'=2] {'block_0'}, dimensions={0} | all-to-all | bytes 262144 | tf_op jit(solution)/shard_map/all_to_all | solution.py:390
  49.5 0.0 copy-start
  49.5 8.1 %all_to_all.37 = f32[4,8,1024]{2,1,0:T(8,128)S(1)} all-to-all(f32[4,8,1024]{2,1,0:T(8,128)S(1)} %broadcast_in_dim.40), channel_id=1, replica_groups=mesh['dp_0'=4,'dp_1'=4,'block_0'=4,'block_1'=4,'block_2'=2] {'dp_0'}, dimensions={0} | all-to-all | bytes 262144 | tf_op jit(solution)/shard_map/all_to_all | solution.py:390
  57.6 10.7 %all_to_all.38.gathered = f32[4,4,8,1024]{3,2,1,0:T(8,128)S(1)} all-to-all(f32[4,4,8,1024]{3,2,1,0:T(8,128)S(1)} %broadcast_in_dim.41), channel_id=1, replica_groups=mesh['dp_0'=4,'dp_1'=4,'block_0'=4,'block_1'=4,'block_2'=2] {'dp_1'}, dimensions={0} | all-to-all | bytes 1048576 | tf_op jit(solution)/shard_map/all_to_all | solution.py:390
  68.4 0.0 copy-done
  68.4 1.4 %shard_map.159 = (f32[64,2048]{1,0:T(8,128)S(1)}, f32[16,72,128]{2,1,0:T(8,128)S(1)}) custom-call(f32[4,4,8,1024]{3,2,1,0:T(8,128)S(1)} %all_to_all.38.gathered, f32[1,128,2048]{2,1,0:T(8,128)S(1)} %copy-done, f32[8,128]{1,0:T(8,128)S(1)} %get-tuple-element.10.predicted), custom_call_target="tpu_custom_call" | custom-call | tf_op jit(solution)/shard_map/pallas_call | solution.py:460
  69.8 15.2 %all_to_all.39.products = f32[16,72,128]{2,1,0:T(8,128)S(1)} all-to-all(f32[16,72,128]{2,1,0:T(8,128)S(1)} %get-tuple-element.12.sent), channel_id=1, replica_groups=mesh['dp_0'=4,'dp_1'=4,'block_0'=4,'block_1'=4,'block_2'=2] {'dp_0','dp_1'}, dimensions={0} | all-to-all | bytes 1179648 | tf_op jit(solution)/shard_map/all_to_all | solution.py:390
  84.9 0.6 shard_map.160
  85.6 15.7 %all_to_all.40.arrived = f32[8,32,128]{2,1,0:T(8,128)S(1)} all-to-all(f32[8,32,128]{2,1,0:T(8,128)S(1)} %shard_map.160), channel_id=1, replica_groups=mesh['dp_0'=4,'dp_1'=4,'block_0'=4,'block_1'=4,'block_2'=2] {'block_1','..., dimensions={0} | all-to-all | bytes 262144 | tf_op jit(solution)/shard_map/all_to_all | solution.py:390
  101.3 14.7 %all_to_all.41.arrived = f32[4,32,128]{2,1,0:T(8,128)S(1)} all-to-all(f32[4,32,128]{2,1,0:T(8,128)S(1)} %shard_map.161), channel_id=1, replica_groups=mesh['dp_0'=4,'dp_1'=4,'block_0'=4,'block_1'=4,'block_2'=2] {'block_0'}, dimensions={0} | all-to-all | bytes 131072 | tf_op jit(solution)/shard_map/all_to_all | solution.py:390
  116.0 3.9 %shard_map.162 = (f32[1,128]{1,0:T(1,128)}, f32[1,128,2048]{2,1,0:T(8,128)}) custom-call(f32[4,32,128]{2,1,0:T(8,128)S(1)} %all_to_all.41.arrived, f32[16,72,128]{2,1,0:T(8,128)S(1)} %all_to_all.39.products, f32[16,72,128]{2,1,0:T(8,128)S(1)} %get-tuple-element.12.sent, f32[1,128,2048]{2,1,0:T(8,128)S(1)} %copy-done, f32[8,128]{1,0:T(8,128)S(1)} %get-tuple-element.13.kept), custom_call_target="tpu_custom_call" | custom-call | tf_op jit(solution)/shard_map/pallas_call | solution.py:486
  (5 shorter events, 0.1 us)
Async XLA Ops:
  5.1 10.3 %collective-permute-start = (f32[4,4,8,1024]{3,2,1,0:T(8,128)S(1)}, f32[4,4,8,1024]{3,2,1,0:T(8,128)S(1)}, u32[]{:S(2)}, u32[]{:S(2)}) collective-permute-start(f32[4,4,8,1024]{3,2,1,0:T(8,128)S(1)} %get-tuple-element.9), channel_id=1, source_target_pairs={{0,1},{1,0},{2,3},{3,2},{4,5},{5,4},{6,7},{7,6},{8,9},{9,8},{10,11... | collective-permute-start | bytes 1572872 | tf_op jit(solution)/shard_map/ppermute | solution.py:455
  49.5 18.9 %copy-start = (f32[1,128,2048]{2,1,0:T(8,128)S(1)}, f32[1,128,2048]{2,1,0:T(8,128)}, u32[]{:S(2)}) copy-start(f32[1,128,2048]{2,1,0:T(8,128)} %covariance.3) | copy-start | bytes 3145732
